TPU v7x, 256 devices: a whole 4x4x8 slice. The times are simulated.
256 devices in a mesh: replica: 16 (over z_lo, y, core), model: 16 (over z_hi, x).
Axes of the slice: x: 4, y: 4, z: 8 (z_hi: 4, z_lo: 2; z = z_hi * 2 + z_lo), core: 2. Of those that a mesh axis runs over, the one named last changes fastest.
Arguments:
- partial_query: float32 [16, 2048, 2048], P('replica', None, 'model'), may hold values from -4 to 4
- partial_key: float32 [16, 2048, 2048], P('replica', None, 'model'), may hold values from -4 to 4
- partial_value: float32 [16, 2048, 2048], P('replica', None, 'model'), may hold values from -4 to 4
- partial_mixed: float32 [16, 2048, 2048], P('replica', 'model'), may hold values from -4 to 4
- partial_norm: float32 [16, 2048], P('replica'), may hold values from -8 to 8
- partial_bias: float32 [16, 2048], P('replica'), may hold values from -8 to 8
- master_query: float32 [2048, 2048], P('replica', 'model'), may hold values from -0.1875 to 0.1875
- master_key: float32 [2048, 2048], P('replica', 'model'), may hold values from -0.1875 to 0.1875
- master_value: float32 [2048, 2048], P('replica', 'model'), may hold values from -0.1875 to 0.1875
- master_mixed: float32 [2048, 2048], P('model', 'replica'), may hold values from -0.1875 to 0.1875
- master_norm: float32 [2048], P('replica'), may hold values from 0.25 to 1.75
- master_bias: float32 [2048], P('replica'), may hold values from -3 to 3
- memory_query: float32 [2048, 2048], P('replica', 'model'), may hold values from 9.765625e-05 to 0.0009765625
- memory_key: float32 [2048, 2048], P('replica', 'model'), may hold values from 9.765625e-05 to 0.0009765625
- memory_value: float32 [2048, 2048], P('replica', 'model'), may hold values from 9.765625e-05 to 0.0009765625
- memory_mixed: float32 [2048, 2048], P('model', 'replica'), may hold values from 9.765625e-05 to 0.0009765625
- memory_norm: float32 [2048], P('replica'), may hold values from 0.05 to 0.8
- memory_bias: float32 [2048], P('replica'), may hold values from 0.05 to 0.8
Outputs:
- compute_query: bfloat16 [2048, 2048], P(None, 'model')
- compute_key: bfloat16 [2048, 2048], P(None, 'model')
- compute_value: bfloat16 [2048, 2048], P(None, 'model')
- compute_mixed: bfloat16 [2048, 2048], P('model')
- compute_norm: bfloat16 [2048], replicated
- compute_bias: bfloat16 [2048], replicated
- stepped_query: float32 [2048, 2048], P('replica', 'model')
- stepped_key: float32 [2048, 2048], P('replica', 'model')
- stepped_value: float32 [2048, 2048], P('replica', 'model')
- stepped_mixed: float32 [2048, 2048], P('model', 'replica')
- stepped_norm: float32 [2048], P('replica')
- stepped_bias: float32 [2048], P('replica')
- state_new_query: float32 [2048, 2048], P('replica', 'model')
- state_new_key: float32 [2048, 2048], P('replica', 'model')
- state_new_value: float32 [2048, 2048], P('replica', 'model')
- state_new_mixed: float32 [2048, 2048], P('model', 'replica')
- state_new_norm: float32 [2048], P('replica')
- state_new_bias: float32 [2048], P('replica')
All inputs are finite; a program needn't handle non-finite values.
Results may differ from a plain program's by a relative error of at most 0.0004.
Values may be sent and summed in bfloat16 or wider, within the bound.
A program may use at most 64 MiB of HBM per device.

v0:
```python
import jax
import jax.numpy as jnp
from jax import lax
from jax.sharding import Mesh
from jax.sharding import PartitionSpec as P

REPLICA = ("replica_0", "replica_1", "replica_2")


learn_rate = 0.015
hold_rate = 0.8


def cut_along(x, dim, size):
    before, after = (x.shape[:dim], x.shape[dim + 1 :])
    return jnp.moveaxis(x.reshape(*before, size, -1, *after), dim, 0)


def sum_at_owner(x, axis, dim):
    size = lax.axis_size(axis)
    blocks = lax.all_to_all(cut_along(x, dim, size), axis, 0, 0, tiled=True)
    return jnp.sum(blocks, axis=0)


def sum_by_axis(x, axes, dim):
    far, near = axes
    own = sum_at_owner(cut_along(x, dim, lax.axis_size(far)), near, dim + 1)
    return jnp.sum(lax.all_to_all(own, far, 0, 0, tiled=True), axis=0)


def in_one_piece(arrays, axis, dim, along):
    widths = [a.shape[along] for a in arrays]
    both = jnp.concatenate(arrays, axis=along)
    out = sum_by_axis(both, axis, dim)
    return tuple(jnp.split(out, [sum(widths[:k]) for k in range(1, len(widths))], axis=along))


def copy_for_each(x, axis):
    copies = jnp.broadcast_to(x, (lax.axis_size(axis), *x.shape))
    return lax.all_to_all(copies, axis, split_axis=0, concat_axis=0, tiled=True)


def of_everyone(x, axis):
    return copy_for_each(x, axis).sum(axis=0)


def together(arrays, axis):
    ends = [0]
    for a in arrays:
        ends.append(ends[-1] + a.size)
    subtotal = of_everyone(jnp.concatenate([a.ravel() for a in arrays]), axis)
    return tuple((subtotal[b:e].reshape(a.shape) for a, b, e in zip(arrays, ends, ends[1:])))


def gather_turned(arrays, axis, dims):
    turned = [jnp.moveaxis(a, dim, 0) for a, dim in zip(arrays, dims)]
    both = jnp.concatenate([t.reshape(len(t), -1) for t in turned], axis=1)
    out, at, outs = (lax.all_gather(both, axis, axis=0, tiled=True), 0, [])
    for t, dim in zip(turned, dims):
        share = out[:, at : at + t[0].size].reshape(-1, *t.shape[1:])
        outs.append(jnp.moveaxis(share, 0, dim))
        at += t[0].size
    return tuple(outs)


def shards(
    partial_query,
    partial_key,
    partial_value,
    partial_mixed,
    partial_norm,
    partial_bias,
    master_query,
    master_key,
    master_value,
    master_mixed,
    master_norm,
    master_bias,
    memory_query,
    memory_key,
    memory_value,
    memory_mixed,
    memory_norm,
    memory_bias,
):
    mean_query, mean_key, mean_value, mean_mixed, mean_norm, mean_bias = (
        *in_one_piece(
            (partial_query[0], partial_key[0], partial_value[0]),
            (("replica_0", "replica_1"), "replica_2"),
            0,
            1,
        ),
        sum_by_axis(partial_mixed[0], (("replica_0", "replica_1"), "replica_2"), 1),
        sum_by_axis(partial_norm[0], (("replica_0", "replica_1"), "replica_2"), 0),
        sum_by_axis(partial_bias[0], (("replica_0", "replica_1"), "replica_2"), 0),
    )
    mean_rate = lax.axis_size(REPLICA) ** (-0.5)
    mean_query = mean_query * mean_rate
    mean_key = mean_key * mean_rate
    mean_value = mean_value * mean_rate
    mean_mixed = mean_mixed * mean_rate
    mean_norm = mean_norm * mean_rate
    mean_bias = mean_bias * mean_rate
    (
        own_query,
        own_key,
        own_value,
        own_mixed,
        slope_query_norm,
        slope_key_norm,
        slope_value_norm,
        slope_mixed_norm,
    ) = together(
        (
            jnp.sum(master_query * master_query, axis=1, keepdims=True),
            jnp.sum(master_key * master_key, axis=1, keepdims=True),
            jnp.sum(master_value * master_value, axis=1, keepdims=True),
            jnp.sum(master_mixed * master_mixed, axis=0, keepdims=True),
            jnp.sum(mean_query * mean_query, axis=1, keepdims=True),
            jnp.sum(mean_key * mean_key, axis=1, keepdims=True),
            jnp.sum(mean_value * mean_value, axis=1, keepdims=True),
            jnp.sum(mean_mixed * mean_mixed, axis=0, keepdims=True),
        ),
        "model",
    )
    mean_query = mean_query * (jnp.sqrt(own_query) * lax.rsqrt(slope_query_norm + 1e-06))
    mean_key = mean_key * (jnp.sqrt(own_key) * lax.rsqrt(slope_key_norm + 1e-06))
    mean_value = mean_value * (jnp.sqrt(own_value) * lax.rsqrt(slope_value_norm + 1e-06))
    mean_mixed = mean_mixed * (jnp.sqrt(own_mixed) * lax.rsqrt(slope_mixed_norm + 1e-06))
    state_new_query = hold_rate * memory_query + (1.0 - hold_rate) * mean_query * mean_query
    stepped_query = master_query - learn_rate * mean_query * lax.rsqrt(state_new_query + 1e-06)
    state_new_key = hold_rate * memory_key + (1.0 - hold_rate) * mean_key * mean_key
    stepped_key = master_key - learn_rate * mean_key * lax.rsqrt(state_new_key + 1e-06)
    state_new_value = hold_rate * memory_value + (1.0 - hold_rate) * mean_value * mean_value
    stepped_value = master_value - learn_rate * mean_value * lax.rsqrt(state_new_value + 1e-06)
    state_new_mixed = hold_rate * memory_mixed + (1.0 - hold_rate) * mean_mixed * mean_mixed
    stepped_mixed = master_mixed - learn_rate * mean_mixed * lax.rsqrt(state_new_mixed + 1e-06)
    state_new_norm = hold_rate * memory_norm + (1.0 - hold_rate) * mean_norm * mean_norm
    stepped_norm = master_norm - learn_rate * mean_norm * lax.rsqrt(state_new_norm + 1e-06)
    state_new_bias = hold_rate * memory_bias + (1.0 - hold_rate) * mean_bias * mean_bias
    stepped_bias = master_bias - learn_rate * mean_bias * lax.rsqrt(state_new_bias + 1e-06)
    compute_query, compute_key, compute_value, compute_mixed, compute_norm, compute_bias = (
        gather_turned(
            (
                stepped_query.astype(jnp.bfloat16),
                stepped_key.astype(jnp.bfloat16),
                stepped_value.astype(jnp.bfloat16),
                stepped_mixed.astype(jnp.bfloat16),
                stepped_norm.astype(jnp.bfloat16),
                stepped_bias.astype(jnp.bfloat16),
            ),
            REPLICA,
            (0, 0, 0, 1, 0, 0),
        )
    )
    return (
        compute_query,
        compute_key,
        compute_value,
        compute_mixed,
        compute_norm,
        compute_bias,
        stepped_query,
        stepped_key,
        stepped_value,
        stepped_mixed,
        stepped_norm,
        stepped_bias,
        state_new_query,
        state_new_key,
        state_new_value,
        state_new_mixed,
        state_new_norm,
        state_new_bias,
    )


def solution(mesh):
    split = Mesh(
        mesh.devices.reshape(2, 4, 2, mesh.shape["model"]),
        ("replica_0", "replica_1", "replica_2", "model"),
    )
    return jax.shard_map(
        shards,
        mesh=split,
        in_specs=(
            P(REPLICA, None, "model"),
            P(REPLICA, None, "model"),
            P(REPLICA, None, "model"),
            P(REPLICA, "model", None),
            P(REPLICA, None),
            P(REPLICA, None),
            P(REPLICA, "model"),
            P(REPLICA, "model"),
            P(REPLICA, "model"),
            P("model", REPLICA),
            P(REPLICA),
            P(REPLICA),
            P(REPLICA, "model"),
            P(REPLICA, "model"),
            P(REPLICA, "model"),
            P("model", REPLICA),
            P(REPLICA),
            P(REPLICA),
        ),
        out_specs=(
            P(None, "model"),
            P(None, "model"),
            P(None, "model"),
            P("model", None),
            P(),
            P(),
            P(REPLICA, "model"),
            P(REPLICA, "model"),
            P(REPLICA, "model"),
            P("model", REPLICA),
            P(REPLICA),
            P(REPLICA),
            P(REPLICA, "model"),
            P(REPLICA, "model"),
            P(REPLICA, "model"),
            P("model", REPLICA),
            P(REPLICA),
            P(REPLICA),
        ),
        check_vma=False,
    )
```

profile of v0, /device:TPU:1, one launch (start us, length us, event | category | flops | bytes accessed | tf_op | source)
XLA Modules:
  0.0 159.4 jit_solution(13763253603055868574)
XLA Ops:
  7.2 1.3 copy.166
  8.5 6.4 %all-to-all-start.5 = ((f32[2,8,128]{2,1,0:T(8,128)}), f32[2,8,128]{2,1,0:T(8,128)S(1)}, u32[]{:S(2)}, u32[]{:S(2)}) async-start(f32[2,8,128]{2,1,0:T(8,128)} %copy.166), calls=%async_computation.5 | async-start | bytes 16384 | tf_op jit(solution)/shard_map/all_to_all | solution.py:21
  14.9 2.1 %maximum_bitcast_fusion = f32[2,8,128,384]{3,2,0,1:T(8,128)S(1)} fusion(f32[8,2,128,128]{3,2,1,0:T(8,128)} %bitcast.29, f32[8,2,128,128]{3,2,1,0:T(8,128)} %bitcast.30, f32[8,2,128,128]{3,2,1,0:T(8,128)} %bitcast.31), kind=kLoop, calls=%fused_computation | loop fusion | flops 1572864 | bytes 6291456 | tf_op jit(solution)/shard_map/transpose | solution.py:16
  17.0 1.9 %copy.142 = f32[2,8,128,384]{3,2,1,0:T(8,128)} copy(f32[2,8,128,384]{3,2,0,1:T(8,128)S(1)} %maximum_bitcast_fusion) | data formatting | bytes 6291456 | tf_op jit(solution)/shard_map/transpose | solution.py:16
  18.9 0.3 copy.146
  19.2 1.3 copy.147
  20.6 4.0 %all-to-all-start = ((f32[2,8,128,384]{3,2,1,0:T(8,128)}), f32[2,8,128,384]{3,2,1,0:T(8,128)S(1)}, u32[]{:S(2)}, u32[]{:S(2)}) async-start(f32[2,8,128,384]{3,2,1,0:T(8,128)} %copy.142), calls=%async_computation | async-start | bytes 6291456 | tf_op jit(solution)/shard_map/all_to_all | solution.py:21
  24.5 0.6 reduce_sum.166
  25.1 2.7 %all-to-all-done = f32[2,8,128,384]{3,2,1,0:T(8,128)S(1)} async-done(((f32[2,8,128,384]{3,2,1,0:T(8,128)}), f32[2,8,128,384]{3,2,1,0:T(8,128)S(1)}, u32[]{:S(2)}, u32[]{:S(2)}) %all-to-all-start) | async-done | bytes 3145760 | tf_op jit(solution)/shard_map/all_to_all | solution.py:21
  27.8 6.6 %all_to_all.54 = f32[2,8,128,128]{3,1,2,0:T(8,128)} all-to-all(f32[2,8,128,128]{3,1,2,0:T(8,128)} %copy.147), channel_id=1, replica_groups=mesh['replica_0'=2,'replica_1'=4,'replica_2'=2,'model'=16] {'replica_2'}, dimensions={0} | all-to-all | bytes 2097152 | tf_op jit(solution)/shard_map/all_to_all | solution.py:21
  34.3 3.7 %all_to_all.55 = f32[2,8,128]{2,1,0:T(8,128)S(1)} all-to-all(f32[2,8,128]{2,1,0:T(8,128)S(1)} %copy.167), channel_id=1, replica_groups=mesh['replica_0'=2,'replica_1'=4,'replica_2'=2,'model'=16] {'replica_2'}, dimensions={0} | all-to-all | bytes 16384 | tf_op jit(solution)/shard_map/all_to_all | solution.py:21
  38.1 3.8 %all-to-all-start.6 = ((f32[8,1,128]{2,1,0:T(1,128)}), f32[8,1,128]{2,1,0:T(1,128)S(1)}, u32[]{:S(2)}, u32[]{:S(2)}) async-start(f32[8,1,128]{2,1,0:T(1,128)} %bitcast.11), calls=%async_computation.6 | async-start | bytes 8192 | tf_op jit(solution)/shard_map/all_to_all | solution.py:28
  41.9 0.6 reduce_sum.168
  42.5 4.4 %all-to-all-done.6 = f32[8,1,128]{2,1,0:T(1,128)S(1)} async-done(((f32[8,1,128]{2,1,0:T(1,128)}), f32[8,1,128]{2,1,0:T(1,128)S(1)}, u32[]{:S(2)}, u32[]{:S(2)}) %all-to-all-start.6) | async-done | bytes 4128 | tf_op jit(solution)/shard_map/all_to_all | solution.py:28
  46.9 3.3 %all-to-all-start.8 = ((f32[8,1,128]{2,1,0:T(1,128)}), f32[8,1,128]{2,1,0:T(1,128)S(1)}, u32[]{:S(2)}, u32[]{:S(2)}) async-start(f32[8,1,128]{2,1,0:T(1,128)} %bitcast.15), calls=%async_computation.8 | async-start | bytes 8192 | tf_op jit(solution)/shard_map/all_to_all | solution.py:28
  50.2 2.1 %reduce_sum.162 = f32[8,128,128]{2,0,1:T(8,128)} reduce(f32[2,8,128,128]{3,1,2,0:T(8,128)} %all_to_all.54, f32[]{:T(128)} %constant.8.clone.1), dimensions={0}, to_apply=%region_9.0 | reduce | flops 131072 | bytes 1572868 | tf_op jit(solution)/shard_map/reduce_sum | solution.py:22
  52.3 1.9 %copy.149 = f32[8,128,128]{2,1,0:T(8,128)} copy(f32[8,128,128]{2,0,1:T(8,128)} %reduce_sum.162) | data formatting | bytes 1048576 | tf_op jit(solution)/shard_map/reduce_sum | solution.py:22
  54.3 0.8 all-to-all-done.8
  55.1 4.3 %all-to-all-start.3 = ((f32[8,128,128]{2,1,0:T(8,128)}), f32[8,128,128]{2,1,0:T(8,128)}, u32[]{:S(2)}, u32[]{:S(2)}) async-start(f32[8,128,128]{2,1,0:T(8,128)} %copy.149), calls=%async_computation.3 | async-start | bytes 1048576 | tf_op jit(solution)/shard_map/all_to_all | solution.py:28
  59.4 1.5 reduce_sum.153
  60.9 5.7 %all-to-all-done.3 = f32[8,128,128]{2,1,0:T(8,128)} async-done(((f32[8,128,128]{2,1,0:T(8,128)}), f32[8,128,128]{2,1,0:T(8,128)}, u32[]{:S(2)}, u32[]{:S(2)}) %all-to-all-start.3) | async-done | bytes 524320 | tf_op jit(solution)/shard_map/all_to_all | solution.py:28
  66.6 3.6 %all-to-all-start.1 = ((f32[8,128,384]{2,1,0:T(8,128)}), f32[8,128,384]{2,1,0:T(8,128)S(1)}, u32[]{:S(2)}, u32[]{:S(2)}) async-start(f32[8,128,384]{2,1,0:T(8,128)} %reduce_sum.153), calls=%async_computation.1 | async-start | bytes 3145728 | tf_op jit(solution)/shard_map/all_to_all | solution.py:28
  70.2 0.1 copy.157
  70.3 0.1 copy.160
  70.4 0.1 copy.154
  70.5 0.1 copy.155
  70.6 0.1 copy.164
  70.7 0.1 copy.165
  70.8 0.1 copy.152
  71.0 0.1 copy.153
  71.0 0.1 multiply_reduce_fusion.7
  71.2 0.1 multiply_reduce_fusion.6
  71.3 0.1 multiply_reduce_fusion.5
  71.5 0.5 convert_bitcast_fusion.2
  72.0 0.1 copy.170
  72.2 1.1 reduce_sum.163
  73.4 0.1 multiply_reduce_fusion
  73.5 13.5 %all-to-all-done.1 = f32[8,128,384]{2,1,0:T(8,128)S(1)} async-done(((f32[8,128,384]{2,1,0:T(8,128)}), f32[8,128,384]{2,1,0:T(8,128)S(1)}, u32[]{:S(2)}, u32[]{:S(2)}) %all-to-all-start.1) | async-done | bytes 1572896 | tf_op jit(solution)/shard_map/all_to_all | solution.py:28
  87.1 0.1 copy.181
  87.3 0.1 copy.182
  87.4 0.1 copy.145
  87.6 0.7 broadcast_in_dim.3
  88.2 9.9 %all-to-all-start.4 = ((f32[16,1,1024]{2,1,0:T(1,128)}), f32[16,1,1024]{2,1,0:T(1,128)S(1)}, u32[]{:S(2)}, u32[]{:S(2)}) async-start(f32[16,1,1024]{2,1,0:T(1,128)} %broadcast_in_dim.3), calls=%async_computation.4 | async-start | bytes 131072 | tf_op jit(solution)/shard_map/all_to_all | solution.py:40
  98.2 0.5 convert_bitcast_fusion.1
  98.7 0.1 copy.171
  98.8 8.2 %all-to-all-done.4 = f32[16,1,1024]{2,1,0:T(1,128)S(1)} async-done(((f32[16,1,1024]{2,1,0:T(1,128)}), f32[16,1,1024]{2,1,0:T(1,128)S(1)}, u32[]{:S(2)}, u32[]{:S(2)}) %all-to-all-start.4) | async-done | bytes 65568 | tf_op jit(solution)/shard_map/all_to_all | solution.py:40
  107.2 0.1 copy.156
  107.3 0.1 copy.159
  107.4 0.1 copy.162
  107.5 0.1 convert_bitcast_fusion
  107.6 0.1 copy.169
  107.8 0.1 copy.168
  107.9 0.8 fusion.3
  108.7 0.8 concatenate.21
  109.4 0.7 copy.174
  110.2 0.7 copy.175
  110.9 0.7 copy.177
  111.6 0.7 copy.178
  112.4 0.7 copy.173
  113.1 0.7 copy.176
  113.8 32.6 %all-gather.2.cloned.1.call-done = bf16[2048,514]{1,0:T(8,128)(2,1)} async-done(((bf16[128,514]{1,0:T(8,128)(2,1)}), bf16[2048,514]{1,0:T(8,128)(2,1)}) %all-gather.2.cloned.1.call-update) | async-done | bytes 2105360 | tf_op jit(solution)/shard_map/all_gather | solution.py:58
  146.4 2.7 %slice_bitcast_fusion = (bf16[128,2048]{0,1:T(8,128)(2,1)S(1)}, bf16[2048,128]{1,0:T(8,128)(2,1)}, bf16[2048,128]{1,0:T(8,128)(2,1)}, bf16[2048,128]{1,0:T(8,128)(2,1)}) fusion(bf16[2048,514]{1,0:T(8,128)(2,1)} %all-gather.2.cloned.1.call-done), kind=kLoop, calls=%fused_computation.3 | loop fusion | bytes 4194304 | tf_op jit(solution)/shard_map/transpose | solution.py:61
  149.1 1.0 copy.172
  150.1 2.5 %slice_reduce_fusion = (bf16[2048]{0:T(1024)(128)(2,1)}, bf16[2048]{0:T(1024)(128)(2,1)}) fusion(bf16[2048,514]{1,0:T(8,128)(2,1)} %all-gather.2.cloned.1.call-done), kind=kLoop, calls=%fused_computation.1 | loop fusion | bytes 16384 | tf_op jit(solution)/shard_map/slice | solution.py:60
  (56 shorter events, 0.8 us)
Async XLA Ops:
  8.5 12.1 %all-to-all-start.5 = ((f32[2,8,128]{2,1,0:T(8,128)}), f32[2,8,128]{2,1,0:T(8,128)S(1)}, u32[]{:S(2)}, u32[]{:S(2)}) async-start(f32[2,8,128]{2,1,0:T(8,128)} %copy.166), calls=%async_computation.5 | async-start | bytes 16384 | tf_op jit(solution)/shard_map/all_to_all | solution.py:21
  17.0 1.9 %copy-start = (f32[1,128,2048]{2,1,0:T(8,128)S(1)}, f32[1,128,2048]{2,1,0:T(8,128)}, u32[]{:S(2)}) copy-start(f32[1,128,2048]{2,1,0:T(8,128)} %param.21) | copy-start | bytes 3145732
  18.9 1.7 %copy-start.9 = (f32[1,2048]{1,0:T(1,128)S(1)}, f32[1,2048]{1,0:T(1,128)}, u32[]{:S(2)}) copy-start(f32[1,2048]{1,0:T(1,128)} %param.23) | copy-start | bytes 24580
  20.6 7.2 %all-to-all-start = ((f32[2,8,128,384]{3,2,1,0:T(8,128)}), f32[2,8,128,384]{3,2,1,0:T(8,128)S(1)}, u32[]{:S(2)}, u32[]{:S(2)}) async-start(f32[2,8,128,384]{3,2,1,0:T(8,128)} %copy.142), calls=%async_computation | async-start | bytes 6291456 | tf_op jit(solution)/shard_map/all_to_all | solution.py:21
  38.1 8.8 %all-to-all-start.6 = ((f32[8,1,128]{2,1,0:T(1,128)}), f32[8,1,128]{2,1,0:T(1,128)S(1)}, u32[]{:S(2)}, u32[]{:S(2)}) async-start(f32[8,1,128]{2,1,0:T(1,128)} %bitcast.11), calls=%async_computation.6 | async-start | bytes 8192 | tf_op jit(solution)/shard_map/all_to_all | solution.py:28
  46.9 8.2 %all-to-all-start.8 = ((f32[8,1,128]{2,1,0:T(1,128)}), f32[8,1,128]{2,1,0:T(1,128)S(1)}, u32[]{:S(2)}, u32[]{:S(2)}) async-start(f32[8,1,128]{2,1,0:T(1,128)} %bitcast.15), calls=%async_computation.8 | async-start | bytes 8192 | tf_op jit(solution)/shard_map/all_to_all | solution.py:28
  55.1 11.5 %all-to-all-start.3 = ((f32[8,128,128]{2,1,0:T(8,128)}), f32[8,128,128]{2,1,0:T(8,128)}, u32[]{:S(2)}, u32[]{:S(2)}) async-start(f32[8,128,128]{2,1,0:T(8,128)} %copy.149), calls=%async_computation.3 | async-start | bytes 1048576 | tf_op jit(solution)/shard_map/all_to_all | solution.py:28
  59.3 10.9 %copy-start.5 = (f32[128,128]{1,0:T(8,128)S(1)}, f32[128,128]{1,0:T(8,128)}, u32[]{:S(2)}) copy-start(f32[128,128]{1,0:T(8,128)} %param.32) | copy-start | bytes 196612
  59.3 11.1 %copy-start.6 = (f32[128,128]{1,0:T(8,128)S(1)}, f32[128,128]{1,0:T(8,128)}, u32[]{:S(2)}) copy-start(f32[128,128]{1,0:T(8,128)} %param.31) | copy-start | bytes 196612
  59.4 11.2 %copy-start.3 = (f32[128,128]{1,0:T(8,128)S(1)}, f32[128,128]{1,0:T(8,128)}, u32[]{:S(2)}) copy-start(f32[128,128]{1,0:T(8,128)} %param.25) | copy-start | bytes 196612
  59.4 11.3 %copy-start.7 = (f32[128,128]{1,0:T(8,128)S(1)}, f32[128,128]{1,0:T(8,128)}, u32[]{:S(2)}) copy-start(f32[128,128]{1,0:T(8,128)} %param.33) | copy-start | bytes 196612
  60.9 9.8 %copy-start.4 = (f32[128,128]{1,0:T(8,128)S(1)}, f32[128,128]{1,0:T(8,128)}, u32[]{:S(2)}) copy-start(f32[128,128]{1,0:T(8,128)} %param.27) | copy-start | bytes 196612
  60.9 9.9 %copy-start.8 = (f32[128,128]{1,0:T(8,128)S(1)}, f32[128,128]{1,0:T(8,128)}, u32[]{:S(2)}) copy-start(f32[128,128]{1,0:T(8,128)} %param.30) | copy-start | bytes 196612
  60.9 10.1 %copy-start.2 = (f32[128,128]{1,0:T(8,128)S(1)}, f32[128,128]{1,0:T(8,128)}, u32[]{:S(2)}) copy-start(f32[128,128]{1,0:T(8,128)} %param.24) | copy-start | bytes 196612
  60.9 10.4 %copy-start.1 = (f32[128,128]{1,0:T(8,128)S(1)}, f32[128,128]{1,0:T(8,128)}, u32[]{:S(2)}) copy-start(f32[128,128]{1,0:T(8,128)} %param.26) | copy-start | bytes 196612
  60.9 10.6 %copy-start.10 = (f32[128]{0:T(128)S(1)}, f32[128]{0:T(128)}, u32[]{:S(2)}) copy-start(f32[128]{0:T(128)} %param.28) | copy-start | bytes 1540
  60.9 10.6 %copy-start.11 = (f32[128]{0:T(128)S(1)}, f32[128]{0:T(128)}, u32[]{:S(2)}) copy-start(f32[128]{0:T(128)} %param.34) | copy-start | bytes 1540
  66.6 20.4 %all-to-all-start.1 = ((f32[8,128,384]{2,1,0:T(8,128)}), f32[8,128,384]{2,1,0:T(8,128)S(1)}, u32[]{:S(2)}, u32[]{:S(2)}) async-start(f32[8,128,384]{2,1,0:T(8,128)} %reduce_sum.153), calls=%async_computation.1 | async-start | bytes 3145728 | tf_op jit(solution)/shard_map/all_to_all | solution.py:28
  70.2 28.0 %copy-start.12 = (f32[128]{0:T(128)S(1)}, f32[128]{0:T(128)}, u32[]{:S(2)}) copy-start(f32[128]{0:T(128)} %param.29) | copy-start | bytes 1540
  70.2 28.0 %copy-start.13 = (f32[128]{0:T(128)S(1)}, f32[128]{0:T(128)}, u32[]{:S(2)}) copy-start(f32[128]{0:T(128)} %param.35) | copy-start | bytes 1540
  88.2 18.8 %all-to-all-start.4 = ((f32[16,1,1024]{2,1,0:T(1,128)}), f32[16,1,1024]{2,1,0:T(1,128)S(1)}, u32[]{:S(2)}, u32[]{:S(2)}) async-start(f32[16,1,1024]{2,1,0:T(1,128)} %broadcast_in_dim.3), calls=%async_computation.4 | async-start | bytes 131072 | tf_op jit(solution)/shard_map/all_to_all | solution.py:40
  98.1 48.3 %all-gather.2.cloned.1.call-start = ((), (), s32[]{:S(2)}) async-start(), calls=%async_computation.9 | async-start | bytes 2785280 | tf_op jit(solution)/shard_map/all_gather | solution.py:58
Sparse Core Ops, SparseCore 0:
  109.6 36.7 all-gather.1
where the time goes:
time: 160 us; the launch traced here: 159 us
  waiting for transfers between devices  67.8 us (42%)
  starting transfers between devices  35.3 us (22%)
  local copies, waits for them, and re-layouts  20.7 us (13%)
  between operations  14.5 us (9%)
  other arithmetic  10.8 us (7%)
  blocking collectives  10.3 us (6%)
    all_gather x1, waiting for transfers between devices, gather_turned(): out, at, outs = (lax.all_gather(both, axis, axis=0, tiled=True), 0, [])  32.6 us
    all_to_all x4, waiting for transfers between devices, sum_by_axis(): return jnp.sum(lax.all_to_all(own, far, 0, 0, tiled=True), axis=0)  24.4 us
    all_to_all x4, starting transfers between devices, sum_by_axis(): return jnp.sum(lax.all_to_all(own, far, 0, 0, tiled=True), axis=0)  15 us
    all_to_all x2, starting transfers between devices, sum_at_owner(): blocks = lax.all_to_all(cut_along(x, dim, size), axis, 0, 0, tiled=True)  10.4 us
    all_to_all x2, blocking collectives, sum_at_owner(): blocks = lax.all_to_all(cut_along(x, dim, size), axis, 0, 0, tiled=True)  10.3 us
    all_to_all x1, starting transfers between devices, copy_for_each(): return lax.all_to_all(copies, axis, split_axis=0, concat_axis=0, tiled=True)  9.85 us
    all_to_all x1, waiting for transfers between devices, copy_for_each(): return lax.all_to_all(copies, axis, split_axis=0, concat_axis=0, tiled=True)  8.2 us
    unnamed x52, local copies, waits for them, and re-layouts  6.61 us
  transfers between devices with their start and end apart: 8, of which 7 were waited for; matrix products, arithmetic and copies ran while one was open for 13% of the time, Pallas kernels for 0%

commit v1 on v0

v1 whole, which is shorter than its diff:
```python
import functools

import jax
import jax.numpy as jnp
from jax import lax
from jax.experimental import pallas as pl
from jax.experimental.pallas import tpu as pltpu
from jax.sharding import PartitionSpec as P

LEARN_RATE = 0.015
HOLD_RATE = 0.8
F32, BF16 = jnp.float32, jnp.bfloat16

CODE_ROWS = 136


def turned(line, to_lanes):
    shape = (128, 128)
    same = lax.broadcasted_iota(jnp.int32, shape, 0) == lax.broadcasted_iota(jnp.int32, shape, 1)
    return jnp.sum(jnp.where(same, line, 0.0), axis=0 if to_lanes else 1, keepdims=True)


def encode(x, i):
    size = jnp.abs(x)
    top = jnp.max(size, axis=0 if i == 3 else 1, keepdims=True)
    top = (top * 1.004 + 1e-30).astype(BF16).astype(F32)
    size = size * (1.0 / top)
    code = jnp.exp2(250.0 * (size * lax.rsqrt(size + 1e-35)) - 125.0)
    code = jnp.where(x < 0, -code, code).astype(BF16)
    line = top if i == 3 else turned(top, True)
    return code, jnp.broadcast_to(line, (CODE_ROWS - 128, 128)).astype(BF16)


def decode(code, line, i):
    code = code.astype(F32)
    line = line.astype(F32)[0:1]
    top = line if i == 3 else turned(line, False)
    root = jnp.log2(jnp.abs(code)) * (1.0 / 250.0) + 0.5
    size = root * root * top
    return jnp.where(code < 0, -size, size)


def update(mean, master, memory):
    state = HOLD_RATE * memory + (1.0 - HOLD_RATE) * mean * mean
    return state, master - LEARN_RATE * mean * lax.rsqrt(state + 1e-06)


def kernel(*refs):
    (pq, pk, pv, pm, pn, pb, *rest) = refs
    masters, small_masters, memories, small_memories, rest = (
        rest[0:4], rest[4:6], rest[6:10], rest[10:12], rest[12:],
    )
    (
        g, stp, sta, sm_g, sm_stp, sm_sta,
        own, pair, snd, rcv, mean, mast, memo,
        sm_own, sm_pair, sm_snd, sm_rcv, sm_mast, sm_memo,
        psnd, prcv,
        own_sem, pair_s, pair_r, rs_s, rs_r, ps_s, ps_r, ag_s, ag_r, rl_s, rl_r,
        in_sem, smo_sem, smp_s, smp_r, smr_s, smr_r,
    ) = rest
    r, m = lax.axis_index("replica"), lax.axis_index("model")
    c = lax.rem(r, 2)
    chip = r // 2
    z, y = chip // 4, lax.rem(chip, 4)
    partner = r + 1 - 2 * c

    def to_chip(k):
        return lax.rem(z + k // 4, 2) * 4 + lax.rem(y + lax.rem(k, 4), 4)

    def from_chip(k):
        return lax.rem(z + k // 4, 2) * 4 + lax.rem(y + 4 - lax.rem(k, 4), 4)

    def remote(src, dst, send, recv, replica, model=None):
        return pltpu.make_async_remote_copy(
            src_ref=src, dst_ref=dst, send_sem=send, recv_sem=recv,
            device_id={"replica": replica, "model": m if model is None else model},
            device_id_type=pl.DeviceIdType.MESH,
        )

    barrier = pltpu.get_barrier_semaphore()

    def hail(replica, model):
        pl.semaphore_signal(
            barrier, inc=1, device_id={"replica": replica, "model": model},
            device_id_type=pl.DeviceIdType.MESH,
        )

    @pl.loop(1, 16)
    def _(j):
        hail(r, lax.rem(m + j, 16))

    @pl.loop(1, 8)
    def _(k):
        hail(2 * to_chip(k) + c, m)

    hail(partner, m)

    def cut(i, d, core):
        if i < 3:
            return (pq, pk, pv)[i].at[d, core]
        return pm.at[:, pl.ds(pl.multiple_of((2 * d + core) * 128, 128), 128)]

    def own_copy(i, d):
        return pltpu.make_async_copy(cut(i, d, c), own.at[i, d], own_sem.at[i, d])

    for i in range(4):
        @pl.loop(0, 8)
        def _(k):
            own_copy(i, to_chip(k)).start()

    small_in = [pltpu.make_async_copy(s, sm_own.at[i], smo_sem.at[i]) for i, s in enumerate((pn, pb))]
    loads = [
        pltpu.make_async_copy(s, d, in_sem.at[n])
        for n, (s, d) in enumerate(
            [(masters[i], mast.at[i]) for i in range(4)]
            + [(memories[i], memo.at[i]) for i in range(4)]
            + [(small_masters[i], sm_mast.at[i]) for i in range(2)]
            + [(small_memories[i], sm_memo.at[i]) for i in range(2)]
        )
    ]
    for copy in small_in + loads:
        copy.start()

    pl.semaphore_wait(barrier, 23)

    def pair_copy(i, d):
        return remote(cut(i, d, 1 - c), pair.at[i, d], pair_s.at[i, d], pair_r.at[i, d], partner)

    small_pair = [remote(s, sm_pair.at[i], smp_s.at[i], smp_r.at[i], partner) for i, s in enumerate((pn, pb))]
    for i in range(4):
        @pl.loop(1, 9)
        def _(k):
            pair_copy(i, to_chip(lax.rem(k, 8))).start()
        if i == 0:
            for copy in small_pair:
                copy.start()

    for copy in loads:
        copy.wait()

    def sizes(x, i):
        x = x * x
        return jnp.sum(x if i == 3 else jnp.transpose(x), axis=0, keepdims=True)

    for i in range(4):
        psnd[i, 1:2, :] = sizes(mast[i], i)

    def rs_copy(i, k):
        return remote(snd.at[i, k - 1], rcv.at[i, k - 1], rs_s.at[i, k - 1], rs_r.at[i, k - 1], 2 * to_chip(k) + c)

    for i in range(4):
        @pl.loop(1, 8)
        def _(k):
            d = to_chip(k)
            own_copy(i, d).wait()
            pair_copy(i, d).wait_recv()
            code, line = encode(own[i, d] + pair[i, d], i)
            snd[i, k - 1, 0:128] = code
            snd[i, k - 1, 128:CODE_ROWS] = line
            rs_copy(i, k).start()

        own_copy(i, chip).wait()
        pair_copy(i, chip).wait_recv()
        mean[i] = own[i, chip] + pair[i, chip]

        if i == 0:
            def small_copy(k):
                return remote(sm_snd.at[2 * to_chip(k) + c], sm_rcv.at[k - 1], smr_s.at[k - 1], smr_r.at[k - 1], 2 * to_chip(k) + c)

            for n in range(2):
                small_in[n].wait()
                small_pair[n].wait_recv()
                line = sm_own[n] + sm_pair[n]
                for b in range(16):
                    sm_snd[b, n : n + 1, :] = line[:, 128 * b : 128 * b + 128]

            @pl.loop(1, 8)
            def _(k):
                small_copy(k).start()

    def psum_copy(i, j):
        return remote(psnd.at[i], prcv.at[i, j - 1], ps_s.at[i, j - 1], ps_r.at[i, j - 1], r, lax.rem(m + j, 16))

    def add_up(i):
        def one(k, total):
            rs_copy(i, k).wait_recv()
            return total + decode(rcv[i, k - 1, 0:128], rcv[i, k - 1, 128:CODE_ROWS], i)

        total = lax.fori_loop(1, 8, one, mean[i]) * 0.25
        mean[i] = total
        psnd[i, 0:1, :] = sizes(total, i)

        @pl.loop(1, 16)
        def _(j):
            psum_copy(i, j).start()

    height = (144, 128, 128, 128)

    def ag_copy(i, k):
        b = g.at[i, r, 0 : height[i]]
        return remote(b, b, ag_s.at[i, k - 1], ag_r.at[i, k - 1], 2 * to_chip(k) + c)

    def relay_copy(i, d):
        b = g.at[i, 2 * d + c, 0 : height[i]]
        return remote(b, b, rl_s.at[i, d], rl_r.at[i, d], partner)

    def step(i):
        def one(j, total):
            psum_copy(i, j).wait_recv()
            return total + prcv[i, j - 1]

        total = lax.fori_loop(1, 16, one, psnd[i])
        ratio = jnp.sqrt(total[1:2]) * lax.rsqrt(total[0:1] + 1e-06)
        ratio = jnp.broadcast_to(ratio, (128, 128))
        if i < 3:
            ratio = jnp.transpose(ratio)
        state, stepped = update(mean[i] * ratio, mast[i], memo[i])
        sta[i] = state
        stp[i] = stepped
        g[i, r, 0:128] = stepped.astype(BF16)

        @pl.loop(1, 8)
        def _(k):
            ag_copy(i, k).start()

        relay_copy(i, chip).start()

    def relay(i):
        @pl.loop(1, 8)
        def _(k):
            ag_copy(i, k).wait_recv()
            relay_copy(i, from_chip(k)).start()

    add_up(0)

    def one(k, total):
        small_copy(k).wait_recv()
        return total + sm_rcv[k - 1]

    total = lax.fori_loop(1, 8, one, sm_snd[r]) * 0.25
    rows = []
    for n in range(2):
        state, stepped = update(total[n : n + 1], sm_mast[n], sm_memo[n])
        sm_sta[n] = state
        sm_stp[n] = stepped
        rows.append(stepped)
    g[0, r, 128:144] = jnp.concatenate(rows + [jnp.zeros((14, 128), F32)], axis=0).astype(BF16)

    add_up(1)
    step(0)
    add_up(2)
    step(1)
    add_up(3)
    relay(0)
    step(2)
    relay(1)
    step(3)

    relay(2)
    relay(3)

    for i in range(4):
        @pl.loop(0, 8)
        def _(d):
            relay_copy(i, d).wait_recv()
        if i == 0:
            for n in range(2):
                rows = [g[0, b, 128:144].astype(F32)[n : n + 1] for b in range(16)]
                sm_g[n] = jnp.concatenate(rows, axis=0).astype(BF16)

    for i in range(4):
        @pl.loop(0, 8)
        def _(d):
            pair_copy(i, d).wait_send()
            relay_copy(i, d).wait_send()

        @pl.loop(1, 8)
        def _(k):
            rs_copy(i, k).wait_send()
            ag_copy(i, k).wait_send()

        @pl.loop(1, 16)
        def _(j):
            psum_copy(i, j).wait_send()

    @pl.loop(1, 8)
    def _(k):
        small_copy(k).wait_send()

    for copy in small_pair:
        copy.wait_send()


def finish(g, stp, sta, sm_g, sm_stp, sm_sta, *rest):
    outs, (sem, mix_sem) = rest[:18], rest[18:]
    pairs = [(g.at[i, :, 0:128], outs[i]) for i in range(3)]
    pairs += [(sm_g.at[n], outs[4 + n]) for n in range(2)]
    pairs += [(stp.at[i], outs[6 + i]) for i in range(4)] + [(sm_stp.at[n], outs[10 + n]) for n in range(2)]
    pairs += [(sta.at[i], outs[12 + i]) for i in range(4)] + [(sm_sta.at[n], outs[16 + n]) for n in range(2)]
    copies = [pltpu.make_async_copy(s, d, sem.at[n]) for n, (s, d) in enumerate(pairs)]
    copies += [
        pltpu.make_async_copy(g.at[3, b, 0:128], outs[3].at[:, 128 * b : 128 * b + 128], mix_sem.at[b]) for b in range(16)
    ]
    for copy in copies:
        copy.start()
    for copy in copies:
        copy.wait()


def shards(*args):
    partials, masters, memories = args[0:6], args[6:12], args[12:18]
    line = lambda a: a.reshape(1, 128)
    operands = (
        *[a.reshape(8, 2, 128, 128) for a in partials[0:3]],
        partials[3].reshape(128, 2048),
        partials[4], partials[5],
        *masters[0:4], *map(line, masters[4:6]),
        *memories[0:4], *map(line, memories[4:6]),
    )
    block = jax.ShapeDtypeStruct((128, 128), F32)
    row = jax.ShapeDtypeStruct((1, 128), F32)
    out_shape = (
        *[jax.ShapeDtypeStruct((16, 128, 128), BF16)] * 3,
        jax.ShapeDtypeStruct((128, 2048), BF16),
        *[jax.ShapeDtypeStruct((16, 128), BF16)] * 2,
        *[block] * 4, *[row] * 2,
        *[block] * 4, *[row] * 2,
    )
    vmem, dma = pltpu.VMEM, pltpu.SemaphoreType.DMA
    held_shape = [
        ((4, 16, 144, 128), BF16), ((4, 128, 128), F32), ((4, 128, 128), F32),
        ((2, 16, 128), BF16), ((2, 1, 128), F32), ((2, 1, 128), F32),
    ]
    held = pl.pallas_call(
        kernel,
        out_shape=[vmem(*a) for a in held_shape],
        in_specs=[pl.BlockSpec(memory_space=pltpu.HBM)] * 18,
        out_specs=[pl.BlockSpec(memory_space=pltpu.VMEM)] * 6,
        scratch_shapes=[
            vmem((4, 8, 128, 128), F32), vmem((4, 8, 128, 128), F32),
            vmem((4, 7, CODE_ROWS, 128), BF16), vmem((4, 7, CODE_ROWS, 128), BF16),
            vmem((4, 128, 128), F32), vmem((4, 128, 128), F32), vmem((4, 128, 128), F32),
            vmem((2, 1, 2048), F32), vmem((2, 1, 2048), F32),
            vmem((16, 2, 128), F32), vmem((7, 2, 128), F32),
            vmem((2, 1, 128), F32), vmem((2, 1, 128), F32),
            vmem((4, 2, 128), F32), vmem((4, 15, 2, 128), F32),
            dma((4, 8)), dma((4, 8)), dma((4, 8)), dma((4, 7)), dma((4, 7)), dma((4, 15)), dma((4, 15)),
            dma((4, 7)), dma((4, 7)), dma((4, 8)), dma((4, 8)),
            dma((12,)), dma((2,)), dma((2,)), dma((2,)), dma((7,)), dma((7,)),
        ],
        compiler_params=pltpu.CompilerParams(collective_id=0, has_side_effects=True, vmem_limit_bytes=62600 * 1024),
    )(*operands)
    outs = pl.pallas_call(
        finish,
        out_shape=out_shape,
        in_specs=[pl.BlockSpec(memory_space=pltpu.VMEM)] * 6,
        out_specs=(pl.BlockSpec(memory_space=pltpu.HBM),) * 18,
        scratch_shapes=[dma((17,)), dma((16,))],
        compiler_params=pltpu.CompilerParams(vmem_limit_bytes=2**20),
    )(*held)
    outs = list(outs)
    for i in range(3):
        outs[i] = outs[i].reshape(2048, 128)
    for i in (4, 5):
        outs[i] = outs[i].reshape(2048)
    for i in (10, 11, 16, 17):
        outs[i] = outs[i].reshape(128)
    return tuple(outs)


def solution(mesh):
    col, row = P("replica", "model"), P("model", "replica")
    per = P("replica")
    return jax.shard_map(
        shards,
        mesh=mesh,
        in_specs=(
            *[P("replica", None, "model")] * 3, P("replica", "model", None), P("replica", None), P("replica", None),
            col, col, col, row, per, per,
            col, col, col, row, per, per,
        ),
        out_specs=(
            *[P(None, "model")] * 3, P("model", None), P(), P(),
            col, col, col, row, per, per,
            col, col, col, row, per, per,
        ),
        check_vma=False,
    )
```

time: 160 us -> 57.5 us (0.36)
  waiting for transfers between devices: 67.8 us -> 0 us
  Pallas kernels: 0 us -> 56.6 us
  starting transfers between devices: 35.3 us -> 0 us
  local copies, waits for them, and re-layouts: 20.7 us -> 0 us
  between operations: 14.5 us -> 0.67 us
  other arithmetic: 10.8 us -> 0 us
  blocking collectives: 10.3 us -> 0 us
    pallas_call x0 -> x2, Pallas kernels: none -> 56.6 us  [the longest x1 54.8 us: shards(): pl.pallas_call(kernel, out_shape=[vmem(*a) for a in held_shape], in_specs...]
    all_to_all x7 -> x0, starting transfers between devices: 35.2 us -> none  [the longest x4 15 us: sum_by_axis(): return jnp.sum(lax.all_to_all(own, far, 0, 0, tiled=True), axis=0)]
    all_to_all x7 -> x0, waiting for transfers between devices: 35.2 us -> none  [the longest x4 24.4 us: sum_by_axis(): return jnp.sum(lax.all_to_all(own, far, 0, 0, tiled=True), axis=0)]
    all_gather x1 -> x0, waiting for transfers between devices: 32.6 us -> none  [gather_turned(): out, at, outs = (lax.all_gather(both, axis, axis=0, tiled=True), 0, [])]
    all_to_all x2 -> x0, blocking collectives: 10.3 us -> none  [sum_at_owner(): blocks = lax.all_to_all(cut_along(x, dim, size), axis, 0, 0, tiled=True)]
    transpose x5 -> x0, local copies, waits for them, and re-layouts: 7.25 us -> none  [the longest x4 4.52 us: cut_along(): return jnp.moveaxis(x.reshape(*before, size, -1, *after), dim, 0)]
    reduce_sum x17 -> x0, other arithmetic: 6.67 us -> none  [the longest x4 4.83 us: sum_at_owner(): return jnp.sum(blocks, axis=0)]
    unnamed x52 -> x0, local copies, waits for them, and re-layouts: 6.61 us -> none
  transfers between devices with their start and end apart: 8 -> 0, of which waited for: 7 -> 0; matrix products, arithmetic and copies ran while one was open for 13% -> 0% of each run, Pallas kernels for 0% -> 0%
where the time goes in v1:
time: 57.5 us; the launch traced here: 57.3 us
  Pallas kernels  56.6 us (98%)
  between operations  0.67 us (1%)
    pallas_call x1, Pallas kernels, shards(): pl.pallas_call(kernel, out_shape=[vmem(*a) for a in held_shape], in_specs...  54.8 us
    pallas_call x1, Pallas kernels, shards(): pl.pallas_call(finish, out_shape=out_shape, in_specs=[pl.BlockSpec(memory...  1.79 us

profile of v1, /device:TPU:1, one launch (start us, length us, event | category | flops | bytes accessed | tf_op | source)
XLA Modules:
  0.0 57.3 jit_solution(4572514552556103963)
XLA Ops:
  0.7 54.8 %shard_map.313 = (bf16[4,16,144,128]{3,2,1,0:T(8,128)(2,1)S(1)}, f32[4,128,128]{2,1,0:T(8,128)S(1)}, f32[4,128,128]{2,1,0:T(8,128)S(1)}, bf16[2,16,128]{2,1,0:T(...) custom-call(f32[8,2,128,128]{3,2,1,0:T(8,128)} %bitcast.17, f32[8,2,128,128]{3,2,1,0:T(8,128)} %bitcast.18, ...), custom_call_target="tpu_custom_call" | custom-call | tf_op jit(solution)/shard_map/pallas_call | solution.py:334
  55.5 1.8 %shard_map.314 = (bf16[16,128,128]{2,1,0:T(8,128)(2,1)}, bf16[16,128,128]{2,1,0:T(8,128)(2,1)}, bf16[16,128,128]{2,1,0:T(8,128)(2,1)}, bf16[128,2048]{1,0:T(8,12...) custom-call(bf16[4,16,144,128]{3,2,1,0:T(8,128)(2,1)S(1)} %get-tuple, ...), custom_call_target="tpu_custom_call" | custom-call | tf_op jit(solution)/shard_map/pallas_call | solution.py:353

commit v2 on v1

v2 whole, which is shorter than its diff:
```python
import functools

import jax
import jax.numpy as jnp
from jax import lax
from jax.experimental import pallas as pl
from jax.experimental.pallas import tpu as pltpu
from jax.sharding import PartitionSpec as P

LEARN_RATE = 0.015
HOLD_RATE = 0.8
F32, BF16 = jnp.float32, jnp.bfloat16

CODE_ROWS = 136


def turned(line, to_lanes):
    shape = (128, 128)
    same = lax.broadcasted_iota(jnp.int32, shape, 0) == lax.broadcasted_iota(jnp.int32, shape, 1)
    return jnp.sum(jnp.where(same, line, 0.0), axis=0 if to_lanes else 1, keepdims=True)


def encode(x, i):
    size = jnp.abs(x)
    top = jnp.max(size, axis=0 if i == 3 else 1, keepdims=True)
    top = (top * 1.004 + 1e-30).astype(BF16).astype(F32)
    size = size * (1.0 / top)
    code = jnp.exp2(250.0 * (size * lax.rsqrt(size + 1e-35)) - 125.0)
    code = jnp.where(x < 0, -code, code).astype(BF16)
    line = top if i == 3 else turned(top, True)
    return code, jnp.broadcast_to(line, (CODE_ROWS - 128, 128)).astype(BF16)


def decode(code, line, i):
    code = code.astype(F32)
    line = line.astype(F32)[0:1]
    top = line if i == 3 else turned(line, False)
    root = jnp.log2(jnp.abs(code)) * (1.0 / 250.0) + 0.5
    size = root * root * top
    return jnp.where(code < 0, -size, size)


def update(mean, master, memory):
    state = HOLD_RATE * memory + (1.0 - HOLD_RATE) * mean * mean
    return state, master - LEARN_RATE * mean * lax.rsqrt(state + 1e-06)


def kernel(*refs):
    (pq, pk, pv, pm, pn, pb, *rest) = refs
    masters, small_masters, memories, small_memories, rest = (
        rest[0:4], rest[4:6], rest[6:10], rest[10:12], rest[12:],
    )
    (
        g, stp, sta, sm_g, sm_stp, sm_sta,
        own, pair, snd, rcv, mean, mast, memo,
        sm_own, sm_pair, sm_snd, sm_rcv, sm_mast, sm_memo,
        psnd, pmid, pxr, pzr,
        own_sem, in_sem, pair_s, first_r, pair_r, smp_s, smp_r, smr_s, smr_r,
        rs_s, rs_r, px_s, px_r, pz_s, pz_r, ag_s, ag_r, last_r, rl_s, rl_r,
    ) = rest
    r, m = lax.axis_index("replica"), lax.axis_index("model")
    c = lax.rem(r, 2)
    chip = r // 2
    z, y = chip // 4, lax.rem(chip, 4)
    partner = r + 1 - 2 * c

    def to_chip(k):
        return lax.rem(z + k // 4, 2) * 4 + lax.rem(y + lax.rem(k, 4), 4)

    def from_chip(k):
        return lax.rem(z + k // 4, 2) * 4 + lax.rem(y + 4 - lax.rem(k, 4), 4)

    def x_peer(j):
        return m // 4 * 4 + lax.rem(m + j, 4)

    def z_peer(j):
        return lax.rem(m + 4 * j, 16)

    def remote(src, dst, send, recv, replica, model=None):
        return pltpu.make_async_remote_copy(
            src_ref=src, dst_ref=dst, send_sem=send, recv_sem=recv,
            device_id={"replica": replica, "model": m if model is None else model},
            device_id_type=pl.DeviceIdType.MESH,
        )

    def wait_bytes(ref, sem):
        pltpu.make_async_copy(ref, ref, sem).wait()

    barrier = pltpu.get_barrier_semaphore()

    def hail(replica, model):
        pl.semaphore_signal(
            barrier, inc=1, device_id={"replica": replica, "model": model},
            device_id_type=pl.DeviceIdType.MESH,
        )

    for j in (2, 1, 3):
        hail(r, z_peer(j))
    for j in (2, 1, 3):
        hail(r, x_peer(j))

    @pl.loop(1, 8)
    def _(k):
        hail(2 * to_chip(k) + c, m)

    hail(partner, m)

    def cut(i, d, core):
        if i < 3:
            return (pq, pk, pv)[i].at[d, core]
        return pm.at[:, pl.ds(pl.multiple_of((2 * d + core) * 128, 128), 128)]

    for i in range(3):
        pltpu.make_async_copy((pq, pk, pv)[i].at[:, c], own.at[i], own_sem.at[i]).start()

    @pl.loop(0, 8)
    def _(d):
        pltpu.make_async_copy(cut(3, d, c), own.at[3, d], own_sem.at[3]).start()

    for i in range(4):
        pltpu.make_async_copy(masters[i], mast.at[i], in_sem.at[0]).start()
        pltpu.make_async_copy(memories[i], memo.at[i], in_sem.at[1]).start()
    for n in range(2):
        pltpu.make_async_copy((pn, pb)[n], sm_own.at[n], in_sem.at[2]).start()
        pltpu.make_async_copy(small_masters[n], sm_mast.at[n], in_sem.at[3]).start()
        pltpu.make_async_copy(small_memories[n], sm_memo.at[n], in_sem.at[4]).start()

    pl.semaphore_wait(barrier, 14)

    def first_copy(d):
        return remote(cut(0, d, 1 - c), pair.at[0, d], pair_s.at[0], first_r.at[d], partner)

    @pl.loop(1, 9)
    def _(k):
        first_copy(to_chip(lax.rem(k, 8))).start()

    for i in (1, 2):
        remote((pq, pk, pv)[i].at[:, 1 - c], pair.at[i], pair_s.at[i], pair_r.at[i - 1], partner).start()
    for n in range(2):
        remote((pn, pb)[n], sm_pair.at[n], smp_s, smp_r, partner).start()

    @pl.loop(0, 8)
    def _(d):
        remote(cut(3, d, 1 - c), pair.at[3, d], pair_s.at[3], pair_r.at[2], partner).start()

    wait_bytes(mast, in_sem.at[0])

    def sizes(x, i):
        x = x * x
        return jnp.sum(x if i == 3 else jnp.transpose(x), axis=0, keepdims=True)

    for i in range(4):
        psnd[i, 1:2, :] = sizes(mast[i], i)

    def rs_copy(i, k):
        return remote(snd.at[i, k - 1], rcv.at[i, k - 1], rs_s, rs_r.at[i], 2 * to_chip(k) + c)

    def code(i, send):
        wait_bytes(own.at[i], own_sem.at[i])
        if i > 0:
            wait_bytes(pair.at[i], pair_r.at[i - 1])

        @pl.loop(1, 8)
        def _(k):
            d = to_chip(k)
            if i == 0:
                first_copy(d).wait_recv()
            snd[i, k - 1, 0:128], snd[i, k - 1, 128:CODE_ROWS] = encode(own[i, d] + pair[i, d], i)
            if send:
                rs_copy(i, k).start()

        if i == 0:
            first_copy(chip).wait_recv()
        mean[i] = own[i, chip] + pair[i, chip]

    def send(i):
        @pl.loop(1, 8)
        def _(k):
            rs_copy(i, k).start()

    def small_copy(k):
        return remote(sm_snd.at[2 * to_chip(k) + c], sm_rcv.at[k - 1], smr_s, smr_r, 2 * to_chip(k) + c)

    def send_small():
        wait_bytes(sm_own, in_sem.at[2])
        wait_bytes(sm_pair, smp_r)
        for n in range(2):
            line = sm_own[n] + sm_pair[n]
            for b in range(16):
                sm_snd[b, n : n + 1, :] = line[:, 128 * b : 128 * b + 128]

        @pl.loop(1, 8)
        def _(k):
            small_copy(k).start()

    def add_up(i):
        wait_bytes(rcv.at[i], rs_r.at[i])

        def one(k, total):
            return total + decode(rcv[i, k, 0:128], rcv[i, k, 128:CODE_ROWS], i)

        total = lax.fori_loop(0, 7, one, mean[i]) * 0.25
        mean[i] = total
        psnd[i, 0:1, :] = sizes(total, i)
        for j in range(1, 4):
            remote(psnd.at[i], pxr.at[i, j - 1], px_s, px_r.at[i], r, x_peer(j)).start()

    def across(i):
        wait_bytes(pxr.at[i], px_r.at[i])
        pmid[i] = psnd[i] + pxr[i, 0] + pxr[i, 1] + pxr[i, 2]
        for j in range(1, 4):
            remote(pmid.at[i], pzr.at[i, j - 1], pz_s, pz_r.at[i], r, z_peer(j)).start()

    height = (144, 128, 128, 128)

    def ag_copy(i, k):
        b = g.at[i, r, 0 : height[i]]
        return remote(b, b, ag_s.at[i], last_r.at[k - 1] if i == 3 else ag_r.at[i], 2 * to_chip(k) + c)

    def relay_copy(i, d):
        b = g.at[i, 2 * d + c, 0 : height[i]]
        return remote(b, b, rl_s.at[i], rl_r.at[i], partner)

    def step(i):
        wait_bytes(pzr.at[i], pz_r.at[i])
        total = pmid[i] + pzr[i, 0] + pzr[i, 1] + pzr[i, 2]
        ratio = jnp.sqrt(total[1:2]) * lax.rsqrt(total[0:1] + 1e-06)
        ratio = jnp.broadcast_to(ratio, (128, 128))
        if i < 3:
            ratio = jnp.transpose(ratio)
        state, stepped = update(mean[i] * ratio, mast[i], memo[i])
        g[i, r, 0:128] = stepped.astype(BF16)
        sta[i] = state
        stp[i] = stepped

        @pl.loop(1, 8)
        def _(k):
            ag_copy(i, k).start()

        relay_copy(i, chip).start()

    def relay(i):
        if i < 3:
            wait_bytes(g.at[i, 0:7, 0 : height[i]], ag_r.at[i])

        @pl.loop(1, 8)
        def _(k):
            if i == 3:
                ag_copy(i, k).wait_recv()
            relay_copy(i, from_chip(k)).start()

    def step_small():
        wait_bytes(sm_rcv, smr_r)
        total = sm_snd[r]
        for k in range(7):
            total = total + sm_rcv[k]
        total = total * 0.25
        wait_bytes(sm_mast, in_sem.at[3])
        wait_bytes(sm_memo, in_sem.at[4])
        rows = []
        for n in range(2):
            state, stepped = update(total[n : n + 1], sm_mast[n], sm_memo[n])
            sm_sta[n] = state
            sm_stp[n] = stepped
            rows.append(stepped)
        g[0, r, 128:144] = jnp.concatenate(rows + [jnp.zeros((14, 128), F32)], axis=0).astype(BF16)

    code(0, True)
    code(1, True)
    send_small()
    code(2, False)
    code(3, False)
    add_up(0)
    send(2)
    step_small()
    wait_bytes(memo, in_sem.at[1])
    across(0)
    add_up(1)
    send(3)
    across(1)
    add_up(2)
    step(0)
    across(2)
    add_up(3)
    step(1)
    across(3)
    relay(0)
    step(2)
    relay(1)
    step(3)
    relay(2)
    relay(3)

    for i in range(4):
        wait_bytes(g.at[i, 0:8, 0 : height[i]], rl_r.at[i])
        if i == 0:
            for n in range(2):
                rows = [g[0, b, 128:144].astype(F32)[n : n + 1] for b in range(16)]
                sm_g[n] = jnp.concatenate(rows, axis=0).astype(BF16)

    for i in range(4):
        wait_bytes(pair.at[i], pair_s.at[i])
        wait_bytes(g.at[i, 0:7, 0 : height[i]], ag_s.at[i])
        wait_bytes(g.at[i, 0:8, 0 : height[i]], rl_s.at[i])
    wait_bytes(sm_pair, smp_s)
    wait_bytes(sm_rcv, smr_s)
    wait_bytes(snd, rs_s)
    wait_bytes(pxr, px_s)
    wait_bytes(pzr, pz_s)


def finish(g, stp, sta, sm_g, sm_stp, sm_sta, *rest):
    outs, sem = rest[:18], rest[18]
    pairs = [(g.at[i, :, 0:128], outs[i]) for i in range(3)]
    pairs += [(g.at[3, b, 0:128], outs[3].at[:, 128 * b : 128 * b + 128]) for b in range(16)]
    pairs += [(sm_g.at[n], outs[4 + n]) for n in range(2)]
    pairs += [(stp.at[i], outs[6 + i]) for i in range(4)] + [(sm_stp.at[n], outs[10 + n]) for n in range(2)]
    pairs += [(sta.at[i], outs[12 + i]) for i in range(4)] + [(sm_sta.at[n], outs[16 + n]) for n in range(2)]
    for src, dst in pairs:
        pltpu.make_async_copy(src, dst, sem).start()
    for src, dst in pairs:
        pltpu.make_async_copy(src, dst, sem).wait()


def shards(*args):
    partials, masters, memories = args[0:6], args[6:12], args[12:18]
    line = lambda a: a.reshape(1, 128)
    operands = (
        *[a.reshape(8, 2, 128, 128) for a in partials[0:3]],
        partials[3].reshape(128, 2048),
        partials[4], partials[5],
        *masters[0:4], *map(line, masters[4:6]),
        *memories[0:4], *map(line, memories[4:6]),
    )
    block = jax.ShapeDtypeStruct((128, 128), F32)
    row = jax.ShapeDtypeStruct((1, 128), F32)
    out_shape = (
        *[jax.ShapeDtypeStruct((16, 128, 128), BF16)] * 3,
        jax.ShapeDtypeStruct((128, 2048), BF16),
        *[jax.ShapeDtypeStruct((16, 128), BF16)] * 2,
        *[block] * 4, *[row] * 2,
        *[block] * 4, *[row] * 2,
    )
    vmem, dma = pltpu.VMEM, pltpu.SemaphoreType.DMA
    held_shape = [
        ((4, 16, 144, 128), BF16), ((4, 128, 128), F32), ((4, 128, 128), F32),
        ((2, 16, 128), BF16), ((2, 1, 128), F32), ((2, 1, 128), F32),
    ]
    held = pl.pallas_call(
        kernel,
        out_shape=[vmem(*a) for a in held_shape],
        in_specs=[pl.BlockSpec(memory_space=pltpu.HBM)] * 18,
        out_specs=[pl.BlockSpec(memory_space=pltpu.VMEM)] * 6,
        scratch_shapes=[
            vmem((4, 8, 128, 128), F32), vmem((4, 8, 128, 128), F32),
            vmem((4, 7, CODE_ROWS, 128), BF16), vmem((4, 7, CODE_ROWS, 128), BF16),
            vmem((4, 128, 128), F32), vmem((4, 128, 128), F32), vmem((4, 128, 128), F32),
            vmem((2, 1, 2048), F32), vmem((2, 1, 2048), F32),
            vmem((16, 2, 128), F32), vmem((7, 2, 128), F32),
            vmem((2, 1, 128), F32), vmem((2, 1, 128), F32),
            vmem((4, 2, 128), F32), vmem((4, 2, 128), F32), vmem((4, 3, 2, 128), F32), vmem((4, 3, 2, 128), F32),
            dma((4,)), dma((5,)), dma((4,)), dma((8,)), dma((3,)), dma, dma, dma, dma,
            dma, dma((4,)), dma, dma((4,)), dma, dma((4,)), dma((4,)), dma((3,)), dma((7,)), dma((4,)), dma((4,)),
        ],
        compiler_params=pltpu.CompilerParams(collective_id=0, has_side_effects=True, vmem_limit_bytes=62600 * 1024),
    )(*operands)
    outs = pl.pallas_call(
        finish,
        out_shape=out_shape,
        in_specs=[pl.BlockSpec(memory_space=pltpu.VMEM)] * 6,
        out_specs=(pl.BlockSpec(memory_space=pltpu.HBM),) * 18,
        scratch_shapes=[dma],
        compiler_params=pltpu.CompilerParams(vmem_limit_bytes=2**20),
    )(*held)
    outs = list(outs)
    for i in range(3):
        outs[i] = outs[i].reshape(2048, 128)
    for i in (4, 5):
        outs[i] = outs[i].reshape(2048)
    for i in (10, 11, 16, 17):
        outs[i] = outs[i].reshape(128)
    return tuple(outs)


def solution(mesh):
    col, row = P("replica", "model"), P("model", "replica")
    per = P("replica")
    return jax.shard_map(
        shards,
        mesh=mesh,
        in_specs=(
            *[P("replica", None, "model")] * 3, P("replica", "model", None), P("replica", None), P("replica", None),
            col, col, col, row, per, per,
            col, col, col, row, per, per,
        ),
        out_specs=(
            *[P(None, "model")] * 3, P("model", None), P(), P(),
            col, col, col, row, per, per,
            col, col, col, row, per, per,
        ),
        check_vma=False,
    )
```

time: 57.5 us -> 47 us (0.82)
  Pallas kernels: 56.6 us -> 46.2 us
    pallas_call x1, Pallas kernels: 54.8 us -> 44.7 us  [shards(): pl.pallas_call(kernel, out_shape=[vmem(*a) for a in held_shape], in_specs...]
where the time goes in v2:
time: 47 us; the launch traced here: 46.8 us
  Pallas kernels  46.2 us (98%)
  between operations  0.67 us (1%)
    pallas_call x1, Pallas kernels, shards(): pl.pallas_call(kernel, out_shape=[vmem(*a) for a in held_shape], in_specs...  44.7 us
    pallas_call x1, Pallas kernels, shards(): pl.pallas_call(finish, out_shape=out_shape, in_specs=[pl.BlockSpec(memory...  1.5 us

profile of v2, /device:TPU:1, one launch (start us, length us, event | category | flops | bytes accessed | tf_op | source)
XLA Modules:
  0.0 46.8 jit_solution(12472357632234918146)
XLA Ops:
  0.7 44.7 %shard_map.313 = (bf16[4,16,144,128]{3,2,1,0:T(8,128)(2,1)S(1)}, f32[4,128,128]{2,1,0:T(8,128)S(1)}, f32[4,128,128]{2,1,0:T(8,128)S(1)}, bf16[2,16,128]{2,1,0:T(...) custom-call(f32[8,2,128,128]{3,2,1,0:T(8,128)} %bitcast.17, f32[8,2,128,128]{3,2,1,0:T(8,128)} %bitcast.18, ...), custom_call_target="tpu_custom_call" | custom-call | tf_op jit(solution)/shard_map/pallas_call | solution.py:349
  45.3 1.5 %shard_map.314 = (bf16[16,128,128]{2,1,0:T(8,128)(2,1)}, bf16[16,128,128]{2,1,0:T(8,128)(2,1)}, bf16[16,128,128]{2,1,0:T(8,128)(2,1)}, bf16[128,2048]{1,0:T(8,12...) custom-call(bf16[4,16,144,128]{3,2,1,0:T(8,128)(2,1)S(1)} %get-tuple, ...), custom_call_target="tpu_custom_call" | custom-call | tf_op jit(solution)/shard_map/pallas_call | solution.py:367

commit v3 on v2

--- a/solution.py
+++ b/solution.py
@@ -12,6 +12,9 @@
 F32, BF16 = jnp.float32, jnp.bfloat16
 
 CODE_ROWS = 136
+
+SUMS = ("direct", "direct", "direct", "direct")
+GATHERS = ("y first", "z first", "y first", "direct")
 
 
 def turned(line, to_lanes):
@@ -31,10 +34,8 @@
     return code, jnp.broadcast_to(line, (CODE_ROWS - 128, 128)).astype(BF16)
 
 
-def decode(code, line, i):
+def decode(code, top):
     code = code.astype(F32)
-    line = line.astype(F32)[0:1]
-    top = line if i == 3 else turned(line, False)
     root = jnp.log2(jnp.abs(code)) * (1.0 / 250.0) + 0.5
     size = root * root * top
     return jnp.where(code < 0, -size, size)
@@ -52,11 +53,11 @@
     )
     (
         g, stp, sta, sm_g, sm_stp, sm_sta,
-        own, pair, snd, rcv, mean, mast, memo,
+        both, pair, snd, rcv, mean, mast, memo,
         sm_own, sm_pair, sm_snd, sm_rcv, sm_mast, sm_memo,
-        psnd, pmid, pxr, pzr,
+        psnd, prcv,
         own_sem, in_sem, pair_s, first_r, pair_r, smp_s, smp_r, smr_s, smr_r,
-        rs_s, rs_r, px_s, px_r, pz_s, pz_r, ag_s, ag_r, last_r, rl_s, rl_r,
+        rs_s, rs_r, fold_r, ps_s, ps_r, near, ag_s, ag_r, rl_s, rl_r,
     ) = rest
     r, m = lax.axis_index("replica"), lax.axis_index("model")
     c = lax.rem(r, 2)
@@ -94,9 +95,9 @@
             device_id_type=pl.DeviceIdType.MESH,
         )
 
-    for j in (2, 1, 3):
+    for j in (1, 3):
         hail(r, z_peer(j))
-    for j in (2, 1, 3):
+    for j in (1, 3):
         hail(r, x_peer(j))
 
     @pl.loop(1, 8)
@@ -105,17 +106,13 @@
 
     hail(partner, m)
 
-    def cut(i, d, core):
-        if i < 3:
-            return (pq, pk, pv)[i].at[d, core]
-        return pm.at[:, pl.ds(pl.multiple_of((2 * d + core) * 128, 128), 128)]
-
     for i in range(3):
-        pltpu.make_async_copy((pq, pk, pv)[i].at[:, c], own.at[i], own_sem.at[i]).start()
-
-    @pl.loop(0, 8)
-    def _(d):
-        pltpu.make_async_copy(cut(3, d, c), own.at[3, d], own_sem.at[3]).start()
+        pltpu.make_async_copy((pq, pk, pv)[i], both.at[i], own_sem.at[i]).start()
+
+    @pl.loop(0, 16)
+    def _(b):
+        cut = pm.at[:, pl.ds(pl.multiple_of(b * 128, 128), 128)]
+        pltpu.make_async_copy(cut, both.at[3, b // 2, lax.rem(b, 2)], own_sem.at[3]).start()
 
     for i in range(4):
         pltpu.make_async_copy(masters[i], mast.at[i], in_sem.at[0]).start()
@@ -125,64 +122,110 @@
         pltpu.make_async_copy(small_masters[n], sm_mast.at[n], in_sem.at[3]).start()
         pltpu.make_async_copy(small_memories[n], sm_memo.at[n], in_sem.at[4]).start()
 
-    pl.semaphore_wait(barrier, 14)
-
-    def first_copy(d):
-        return remote(cut(0, d, 1 - c), pair.at[0, d], pair_s.at[0], first_r.at[d], partner)
-
-    @pl.loop(1, 9)
-    def _(k):
-        first_copy(to_chip(lax.rem(k, 8))).start()
-
-    for i in (1, 2):
-        remote((pq, pk, pv)[i].at[:, 1 - c], pair.at[i], pair_s.at[i], pair_r.at[i - 1], partner).start()
-    for n in range(2):
-        remote((pn, pb)[n], sm_pair.at[n], smp_s, smp_r, partner).start()
-
-    @pl.loop(0, 8)
-    def _(d):
-        remote(cut(3, d, 1 - c), pair.at[3, d], pair_s.at[3], pair_r.at[2], partner).start()
-
-    wait_bytes(mast, in_sem.at[0])
-
     def sizes(x, i):
         x = x * x
         return jnp.sum(x if i == 3 else jnp.transpose(x), axis=0, keepdims=True)
 
-    for i in range(4):
-        psnd[i, 1:2, :] = sizes(mast[i], i)
+    wait_bytes(both.at[0], own_sem.at[0])
+    pl.semaphore_wait(barrier, 12)
+
+    def tell(peer, n):
+        for j in (1, 3):
+            pl.semaphore_signal(
+                near.at[n], inc=1, device_id={"replica": r, "model": peer(j)}, device_id_type=pl.DeviceIdType.MESH
+            )
+
+    tell(z_peer, 0)
+
+    def first_copy(d):
+        return remote(both.at[0, d, 1 - c], pair.at[0, d], pair_s.at[0], first_r.at[d], partner)
+
+    @pl.loop(1, 9)
+    def _(n):
+        first_copy(to_chip(8 - n)).start()
+
+    wait_bytes(sm_own, in_sem.at[2])
+    for n in range(2):
+        remote(sm_own.at[n], sm_pair.at[n], smp_s, smp_r, partner).start()
+    for i in range(1, 4):
+        wait_bytes(both.at[i], own_sem.at[i])
+        remote(both.at[i, :, 1 - c], pair.at[i], pair_s.at[i], pair_r.at[i - 1], partner).start()
+
+    def prepare():
+        pl.semaphore_wait(near.at[1], 2)
+        tell(x_peer, 2)
+        wait_bytes(mast, in_sem.at[0])
+        for i in range(4):
+            psnd[i, 1:2, :] = sizes(mast[i], i)
+        wait_bytes(memo, in_sem.at[1])
+        wait_bytes(sm_mast, in_sem.at[3])
+        wait_bytes(sm_memo, in_sem.at[4])
+
+    def terms(i, d):
+        return both[i, d, c] + pair[i, d]
 
     def rs_copy(i, k):
-        return remote(snd.at[i, k - 1], rcv.at[i, k - 1], rs_s, rs_r.at[i], 2 * to_chip(k) + c)
+        late = isinstance(k, int) and SUMS[i] != "direct"
+        if SUMS[i] == "direct":
+            at = to_chip(k)
+        elif SUMS[i] == "z first":
+            at = to_chip(4) if not isinstance(k, int) else to_chip(k)
+        else:
+            at = to_chip(lax.rem(k, 4)) if not isinstance(k, int) else to_chip(k)
+        return remote(snd.at[i, k - 1], rcv.at[i, k - 1], rs_s, (fold_r if late else rs_r).at[i], 2 * at + c)
+
+    def code_block(i, k, x):
+        snd[i, k - 1, 0:128], snd[i, k - 1, 128:CODE_ROWS] = encode(x, i)
+
+    def early(i):
+        return {"direct": ((1, 8),), "z first": ((4, 8),), "y first": ((5, 8), (1, 4))}[SUMS[i]]
 
     def code(i, send):
-        wait_bytes(own.at[i], own_sem.at[i])
         if i > 0:
             wait_bytes(pair.at[i], pair_r.at[i - 1])
 
-        @pl.loop(1, 8)
-        def _(k):
-            d = to_chip(k)
-            if i == 0:
-                first_copy(d).wait_recv()
-            snd[i, k - 1, 0:128], snd[i, k - 1, 128:CODE_ROWS] = encode(own[i, d] + pair[i, d], i)
-            if send:
-                rs_copy(i, k).start()
+        for lo, hi in early(i):
+            @pl.loop(0, hi - lo)
+            def _(n):
+                k = hi - 1 - n
+                d = to_chip(k)
+                if i == 0:
+                    first_copy(d).wait_recv()
+                code_block(i, k, terms(i, d))
+                if send:
+                    rs_copy(i, k).start()
 
         if i == 0:
             first_copy(chip).wait_recv()
-        mean[i] = own[i, chip] + pair[i, chip]
+        mean[i] = terms(i, chip)
 
     def send(i):
-        @pl.loop(1, 8)
-        def _(k):
-            rs_copy(i, k).start()
+        for lo, hi in early(i):
+            @pl.loop(0, hi - lo)
+            def _(n):
+                rs_copy(i, hi - 1 - n).start()
+
+    def heard(i, k):
+        line = rcv[i, k - 1, 128:CODE_ROWS].astype(F32)[0:1]
+        return decode(rcv[i, k - 1, 0:128], line if i == 3 else turned(line, False))
+
+    def fold(i):
+        if SUMS[i] == "z first":
+            wait_bytes(rcv.at[i, 0:4], rs_r.at[i])
+            for k in (2, 1, 3):
+                d = to_chip(k)
+                code_block(i, k, terms(i, d) + heard(i, 4 + k))
+                rs_copy(i, k).start()
+        else:
+            wait_bytes(rcv.at[i, 0:6], rs_r.at[i])
+            d = to_chip(4)
+            code_block(i, 4, terms(i, d) + heard(i, 5) + heard(i, 6) + heard(i, 7))
+            rs_copy(i, 4).start()
 
     def small_copy(k):
         return remote(sm_snd.at[2 * to_chip(k) + c], sm_rcv.at[k - 1], smr_s, smr_r, 2 * to_chip(k) + c)
 
     def send_small():
-        wait_bytes(sm_own, in_sem.at[2])
         wait_bytes(sm_pair, smp_r)
         for n in range(2):
             line = sm_own[n] + sm_pair[n]
@@ -194,36 +237,45 @@
             small_copy(k).start()
 
     def add_up(i):
-        wait_bytes(rcv.at[i], rs_r.at[i])
-
-        def one(k, total):
-            return total + decode(rcv[i, k, 0:128], rcv[i, k, 128:CODE_ROWS], i)
-
-        total = lax.fori_loop(0, 7, one, mean[i]) * 0.25
+        if SUMS[i] == "direct":
+            wait_bytes(rcv.at[i], rs_r.at[i])
+        else:
+            last = 3 if SUMS[i] == "z first" else 1
+            wait_bytes(rcv.at[i, 0:last], fold_r.at[i])
+
+        n = 7 if SUMS[i] == "direct" else 4
+        lines = [rcv[i, k, 128:CODE_ROWS].astype(F32)[0:1] for k in range(n)]
+        if i < 3:
+            whole = jnp.transpose(jnp.concatenate(lines + [jnp.zeros((128 - n, 128), F32)], axis=0))
+            lines = [whole[:, k : k + 1] for k in range(n)]
+        total = mean[i]
+        for k in range(n):
+            total = total + decode(rcv[i, k, 0:128], lines[k])
+        total = total * 0.25
         mean[i] = total
         psnd[i, 0:1, :] = sizes(total, i)
-        for j in range(1, 4):
-            remote(psnd.at[i], pxr.at[i, j - 1], px_s, px_r.at[i], r, x_peer(j)).start()
-
-    def across(i):
-        wait_bytes(pxr.at[i], px_r.at[i])
-        pmid[i] = psnd[i] + pxr[i, 0] + pxr[i, 1] + pxr[i, 2]
-        for j in range(1, 4):
-            remote(pmid.at[i], pzr.at[i, j - 1], pz_s, pz_r.at[i], r, z_peer(j)).start()
+        if i == 0:
+            pl.semaphore_wait(near.at[2], 2)
+
+        @pl.loop(1, 16)
+        def _(j):
+            remote(psnd.at[i], prcv.at[i, j - 1], ps_s, ps_r.at[i], r, lax.rem(m + j, 16)).start()
 
     height = (144, 128, 128, 128)
 
-    def ag_copy(i, k):
-        b = g.at[i, r, 0 : height[i]]
-        return remote(b, b, ag_s.at[i], last_r.at[k - 1] if i == 3 else ag_r.at[i], 2 * to_chip(k) + c)
+    def ag_copy(i, d, k, group):
+        b = g.at[i, 2 * d + c, 0 : height[i]]
+        return remote(b, b, ag_s.at[i], ag_r.at[i, group], 2 * to_chip(k) + c)
 
     def relay_copy(i, d):
         b = g.at[i, 2 * d + c, 0 : height[i]]
         return remote(b, b, rl_s.at[i], rl_r.at[i], partner)
 
     def step(i):
-        wait_bytes(pzr.at[i], pz_r.at[i])
-        total = pmid[i] + pzr[i, 0] + pzr[i, 1] + pzr[i, 2]
+        wait_bytes(prcv.at[i], ps_r.at[i])
+        total = psnd[i]
+        for j in range(15):
+            total = total + prcv[i, j]
         ratio = jnp.sqrt(total[1:2]) * lax.rsqrt(total[0:1] + 1e-06)
         ratio = jnp.broadcast_to(ratio, (128, 128))
         if i < 3:
@@ -233,21 +285,51 @@
         sta[i] = state
         stp[i] = stepped
 
-        @pl.loop(1, 8)
+        for group, (lo, hi) in ((2, (5, 8)), (1, (4, 5)), (0, (1, 4))):
+            if group == 2 and GATHERS[i] != "direct":
+                continue
+
+            @pl.loop(lo, hi)
+            def _(k):
+                ag_copy(i, chip, k, group).start()
+
+        relay_copy(i, chip).start()
+
+    def arrive(i, group):
+        n = (3, 1, 3)[group]
+        wait_bytes(g.at[i, 0:n, 0 : height[i]], ag_r.at[i, group])
+
+    def pass_on(i, group):
+        lo, hi = ((1, 4), (4, 5), (5, 8))[group]
+
+        @pl.loop(lo, hi)
         def _(k):
-            ag_copy(i, k).start()
-
-        relay_copy(i, chip).start()
+            relay_copy(i, from_chip(k)).start()
+
+    def forward(i):
+        if GATHERS[i] == "z first":
+            arrive(i, 1)
+
+            @pl.loop(1, 4)
+            def _(k):
+                ag_copy(i, from_chip(4), k, 2).start()
+
+            pass_on(i, 1)
+        if GATHERS[i] == "y first":
+            arrive(i, 0)
+
+            @pl.loop(1, 4)
+            def _(k):
+                ag_copy(i, from_chip(k), 4, 2).start()
+
+            pass_on(i, 0)
 
     def relay(i):
-        if i < 3:
-            wait_bytes(g.at[i, 0:7, 0 : height[i]], ag_r.at[i])
-
-        @pl.loop(1, 8)
-        def _(k):
-            if i == 3:
-                ag_copy(i, k).wait_recv()
-            relay_copy(i, from_chip(k)).start()
+        for group in (0, 1, 2):
+            if group == {"z first": 1, "y first": 0, "direct": None}[GATHERS[i]]:
+                continue
+            arrive(i, group)
+            pass_on(i, group)
 
     def step_small():
         wait_bytes(sm_rcv, smr_r)
@@ -255,8 +337,6 @@
         for k in range(7):
             total = total + sm_rcv[k]
         total = total * 0.25
-        wait_bytes(sm_mast, in_sem.at[3])
-        wait_bytes(sm_memo, in_sem.at[4])
         rows = []
         for n in range(2):
             state, stepped = update(total[n : n + 1], sm_mast[n], sm_memo[n])
@@ -266,28 +346,28 @@
         g[0, r, 128:144] = jnp.concatenate(rows + [jnp.zeros((14, 128), F32)], axis=0).astype(BF16)
 
     code(0, True)
+    pl.semaphore_wait(near.at[0], 2)
+    tell(x_peer, 1)
+    send_small()
     code(1, True)
-    send_small()
-    code(2, False)
+    prepare()
+    code(2, True)
     code(3, False)
     add_up(0)
-    send(2)
+    send(3)
     step_small()
-    wait_bytes(memo, in_sem.at[1])
-    across(0)
     add_up(1)
-    send(3)
-    across(1)
     add_up(2)
+    add_up(3)
     step(0)
-    across(2)
-    add_up(3)
     step(1)
-    across(3)
+    step(2)
+    forward(0)
+    forward(1)
+    step(3)
+    forward(2)
     relay(0)
-    step(2)
     relay(1)
-    step(3)
     relay(2)
     relay(3)
 
@@ -305,8 +385,7 @@
     wait_bytes(sm_pair, smp_s)
     wait_bytes(sm_rcv, smr_s)
     wait_bytes(snd, rs_s)
-    wait_bytes(pxr, px_s)
-    wait_bytes(pzr, pz_s)
+    wait_bytes(prcv, ps_s)
 
 
 def finish(g, stp, sta, sm_g, sm_stp, sm_sta, *rest):
@@ -352,15 +431,16 @@
         in_specs=[pl.BlockSpec(memory_space=pltpu.HBM)] * 18,
         out_specs=[pl.BlockSpec(memory_space=pltpu.VMEM)] * 6,
         scratch_shapes=[
-            vmem((4, 8, 128, 128), F32), vmem((4, 8, 128, 128), F32),
+            vmem((4, 8, 2, 128, 128), F32), vmem((4, 8, 128, 128), F32),
             vmem((4, 7, CODE_ROWS, 128), BF16), vmem((4, 7, CODE_ROWS, 128), BF16),
             vmem((4, 128, 128), F32), vmem((4, 128, 128), F32), vmem((4, 128, 128), F32),
             vmem((2, 1, 2048), F32), vmem((2, 1, 2048), F32),
             vmem((16, 2, 128), F32), vmem((7, 2, 128), F32),
             vmem((2, 1, 128), F32), vmem((2, 1, 128), F32),
-            vmem((4, 2, 128), F32), vmem((4, 2, 128), F32), vmem((4, 3, 2, 128), F32), vmem((4, 3, 2, 128), F32),
+            vmem((4, 2, 128), F32), vmem((4, 15, 2, 128), F32),
             dma((4,)), dma((5,)), dma((4,)), dma((8,)), dma((3,)), dma, dma, dma, dma,
-            dma, dma((4,)), dma, dma((4,)), dma, dma((4,)), dma((4,)), dma((3,)), dma((7,)), dma((4,)), dma((4,)),
+            dma, dma((4,)), dma((4,)), dma, dma((4,)), pltpu.SemaphoreType.REGULAR((3,)),
+            dma((4,)), dma((4, 3)), dma((4,)), dma((4,)),
         ],
         compiler_params=pltpu.CompilerParams(collective_id=0, has_side_effects=True, vmem_limit_bytes=62600 * 1024),
     )(*operands)

time: 47 us -> 44.3 us (0.943)
  Pallas kernels: 46.2 us -> 43.5 us
    pallas_call x1, Pallas kernels: 44.7 us -> 42 us  [shards(): pl.pallas_call(kernel, out_shape=[vmem(*a) for a in held_shape], in_specs...]
where the time goes in v3:
time: 44.3 us; the launch traced here: 44.2 us
  Pallas kernels  43.5 us (98%)
  between operations  0.67 us (2%)
    pallas_call x1, Pallas kernels, shards(): pl.pallas_call(kernel, out_shape=[vmem(*a) for a in held_shape], in_specs...  42 us
    pallas_call x1, Pallas kernels, shards(): pl.pallas_call(finish, out_shape=out_shape, in_specs=[pl.BlockSpec(memory...  1.5 us

profile of v3, /device:TPU:1, one launch (start us, length us, event | category | flops | bytes accessed | tf_op | source)
XLA Modules:
  0.0 44.2 jit_solution(8611168394362299122)
XLA Ops:
  0.7 42.0 %shard_map.313 = (bf16[4,16,144,128]{3,2,1,0:T(8,128)(2,1)S(1)}, f32[4,128,128]{2,1,0:T(8,128)S(1)}, f32[4,128,128]{2,1,0:T(8,128)S(1)}, bf16[2,16,128]{2,1,0:T(...) custom-call(f32[8,2,128,128]{3,2,1,0:T(8,128)} %bitcast.17, f32[8,2,128,128]{3,2,1,0:T(8,128)} %bitcast.18, ...), custom_call_target="tpu_custom_call" | custom-call | tf_op jit(solution)/shard_map/pallas_call | solution.py:428
  42.7 1.5 %shard_map.314 = (bf16[16,128,128]{2,1,0:T(8,128)(2,1)}, bf16[16,128,128]{2,1,0:T(8,128)(2,1)}, bf16[16,128,128]{2,1,0:T(8,128)(2,1)}, bf16[128,2048]{1,0:T(8,12...) custom-call(bf16[4,16,144,128]{3,2,1,0:T(8,128)(2,1)S(1)} %get-tuple, ...), custom_call_target="tpu_custom_call" | custom-call | tf_op jit(solution)/shard_map/pallas_call | solution.py:447

commit v4 on v3

v4 whole, which is shorter than its diff:
```python
import functools

import jax
import jax.numpy as jnp
from jax import lax
from jax.experimental import pallas as pl
from jax.experimental.pallas import tpu as pltpu
from jax.sharding import PartitionSpec as P

LEARN_RATE = 0.015
HOLD_RATE = 0.8
F32, BF16 = jnp.float32, jnp.bfloat16

PIECES = ((3, 0, 128), (0, 0, 64), (0, 64, 128), (1, 0, 64), (1, 64, 128), (2, 0, 64), (2, 64, 128))
WITH_SMALL = 2
GATHERS = ("direct", "y first", "z first", "direct", "direct", "direct", "direct")


def encode(x, i):
    rows = x.shape[0]
    size = jnp.abs(x)
    top = jnp.max(size, axis=0 if i == 3 else 1, keepdims=True)
    top = (top * 1.004 + 1e-30).astype(BF16).astype(F32)
    size = size * (1.0 / top)
    code = jnp.exp2(250.0 * (size * lax.rsqrt(size + 1e-35)) - 125.0)
    code = jnp.where(x < 0, -code, code).astype(BF16)
    if i < 3:
        shape = (rows, 128)
        same = lax.broadcasted_iota(jnp.int32, shape, 0) == lax.broadcasted_iota(jnp.int32, shape, 1)
        top = jnp.sum(jnp.where(same, top, 0.0), axis=0, keepdims=True)
    return code, jnp.broadcast_to(top, (8, 128)).astype(BF16)


def decode(code, top):
    code = code.astype(F32)
    root = jnp.log2(jnp.abs(code)) * (1.0 / 250.0) + 0.5
    size = root * root * top
    return jnp.where(code < 0, -size, size)


def update(mean, master, memory):
    state = HOLD_RATE * memory + (1.0 - HOLD_RATE) * mean * mean
    return state, master - LEARN_RATE * mean * lax.rsqrt(state + 1e-06)


def kernel(*refs):
    (pq, pk, pv, pm, pn, pb, *rest) = refs
    masters, small_masters, memories, small_memories, rest = (
        rest[0:4], rest[4:6], rest[6:10], rest[10:12], rest[12:],
    )
    (
        g, stp, sta, sm_g, sm_stp, sm_sta,
        both, pair, snd, rcv, mean, mast, memo,
        sm_own, sm_pair, sm_snd, sm_rcv, sm_mast, sm_memo,
        psnd, prcv,
        own_sem, in_sem, pair_s, first_r, pair_r, smp_s, smp_r, smr_s, smr_r,
        rs_s, rs_r, ps_s, ps_r, near, ag_s, ag_r, rl_s, rl_r,
    ) = rest
    r, m = lax.axis_index("replica"), lax.axis_index("model")
    c = lax.rem(r, 2)
    chip = r // 2
    z, y = chip // 4, lax.rem(chip, 4)
    partner = r + 1 - 2 * c

    def to_chip(k):
        return lax.rem(z + k // 4, 2) * 4 + lax.rem(y + lax.rem(k, 4), 4)

    def from_chip(k):
        return lax.rem(z + k // 4, 2) * 4 + lax.rem(y + 4 - lax.rem(k, 4), 4)

    def x_peer(j):
        return m // 4 * 4 + lax.rem(m + j, 4)

    def z_peer(j):
        return lax.rem(m + 4 * j, 16)

    def remote(src, dst, send, recv, replica, model=None):
        return pltpu.make_async_remote_copy(
            src_ref=src, dst_ref=dst, send_sem=send, recv_sem=recv,
            device_id={"replica": replica, "model": m if model is None else model},
            device_id_type=pl.DeviceIdType.MESH,
        )

    def wait_bytes(ref, sem):
        pltpu.make_async_copy(ref, ref, sem).wait()

    barrier = pltpu.get_barrier_semaphore()

    def hail(replica, model):
        pl.semaphore_signal(
            barrier, inc=1, device_id={"replica": replica, "model": model},
            device_id_type=pl.DeviceIdType.MESH,
        )

    for j in (1, 3):
        hail(r, z_peer(j))
    for j in (1, 3):
        hail(r, x_peer(j))

    @pl.loop(1, 8)
    def _(k):
        hail(2 * to_chip(k) + c, m)

    hail(partner, m)

    @pl.loop(0, 16)
    def _(b):
        cut = pm.at[:, pl.ds(pl.multiple_of(b * 128, 128), 128)]
        pltpu.make_async_copy(cut, both.at[3, b // 2, lax.rem(b, 2)], own_sem.at[3]).start()

    for i in range(3):
        pltpu.make_async_copy((pq, pk, pv)[i], both.at[i], own_sem.at[i]).start()
    for i in range(4):
        pltpu.make_async_copy(masters[i], mast.at[i], in_sem.at[0]).start()
        pltpu.make_async_copy(memories[i], memo.at[i], in_sem.at[1]).start()
    for n in range(2):
        pltpu.make_async_copy((pn, pb)[n], sm_own.at[n], in_sem.at[2]).start()
        pltpu.make_async_copy(small_masters[n], sm_mast.at[n], in_sem.at[3]).start()
        pltpu.make_async_copy(small_memories[n], sm_memo.at[n], in_sem.at[4]).start()

    def sizes(x, i):
        x = x * x
        return jnp.sum(x if i == 3 else jnp.transpose(x), axis=0, keepdims=True)

    wait_bytes(both.at[3], own_sem.at[3])
    pl.semaphore_wait(barrier, 12)

    def tell(peer, n):
        for j in (1, 3):
            pl.semaphore_signal(
                near.at[n], inc=1, device_id={"replica": r, "model": peer(j)}, device_id_type=pl.DeviceIdType.MESH
            )

    tell(z_peer, 0)

    def first_copy(d):
        return remote(both.at[3, d, 1 - c], pair.at[3, d], pair_s.at[3], first_r.at[d], partner)

    @pl.loop(1, 9)
    def _(n):
        first_copy(to_chip(8 - n)).start()

    wait_bytes(sm_own, in_sem.at[2])
    for n in range(2):
        remote(sm_own.at[n], sm_pair.at[n], smp_s, smp_r, partner).start()
    for i in range(3):
        wait_bytes(both.at[i], own_sem.at[i])
        remote(both.at[i, :, 1 - c], pair.at[i], pair_s.at[i], pair_r.at[i], partner).start()

    def prepare():
        pl.semaphore_wait(near.at[1], 2)
        tell(x_peer, 2)
        wait_bytes(mast, in_sem.at[0])
        psnd[...] = jnp.zeros_like(psnd)
        for p, (i, lo, hi) in enumerate(PIECES):
            psnd[p, 1:2, 0 : hi - lo] = sizes(mast[i, lo:hi], i)
        wait_bytes(memo, in_sem.at[1])
        wait_bytes(sm_mast, in_sem.at[3])
        wait_bytes(sm_memo, in_sem.at[4])

    def terms(p, d):
        i, lo, hi = PIECES[p]
        return both[i, d, c, lo:hi] + pair[i, d, lo:hi]

    def rs_copy(p, k):
        rows = PIECES[p][2] - PIECES[p][1] + 8
        src, dst = snd.at[p, k - 1, 0:rows], rcv.at[p, k - 1, 0:rows]
        return remote(src, dst, rs_s.at[p], rs_r.at[p], 2 * to_chip(k) + c)

    def code(p, send):
        i, lo, hi = PIECES[p]
        if p > 0 and lo == 0:
            wait_bytes(pair.at[i], pair_r.at[i])

        rows = hi - lo
        for group in ((7, 6), (5, 4), (3, 2), (1,)) if p == 0 else ((7, 6, 5, 4), (3, 2, 1)):
            if p == 0:
                for k in group:
                    first_copy(to_chip(k)).wait_recv()
            codes = [encode(terms(p, to_chip(k)), i) for k in group]
            for k, (values, tops) in zip(group, codes):
                snd[p, k - 1, 0:rows] = values
                snd[p, k - 1, rows : rows + 8] = tops
            if send:
                for k in group:
                    rs_copy(p, k).start()

        if p == 0:
            first_copy(chip).wait_recv()
        mean[i, lo:hi] = terms(p, chip)

    def send(p):
        @pl.loop(0, 7)
        def _(n):
            rs_copy(p, 7 - n).start()

    def small_copy(k):
        return remote(sm_snd.at[2 * to_chip(k) + c], sm_rcv.at[k - 1], smr_s, smr_r, 2 * to_chip(k) + c)

    def send_small():
        wait_bytes(sm_pair, smp_r)
        for n in range(2):
            line = sm_own[n] + sm_pair[n]
            for b in range(16):
                sm_snd[b, n : n + 1, :] = line[:, 128 * b : 128 * b + 128]

        @pl.loop(1, 8)
        def _(k):
            small_copy(k).start()

    def add_up(p):
        i, lo, hi = PIECES[p]
        rows = hi - lo
        wait_bytes(rcv.at[p, :, 0 : rows + 8], rs_r.at[p])
        tops = [rcv[p, k, rows : rows + 8].astype(F32)[0:1] for k in range(7)]
        if i < 3:
            whole = jnp.transpose(jnp.concatenate(tops + [jnp.zeros((121, 128), F32)], axis=0))
            tops = [whole[0:rows, k : k + 1] for k in range(7)]
        total = mean[i, lo:hi]
        for k in range(7):
            total = total + decode(rcv[p, k, 0:rows], tops[k])
        total = total * 0.25
        mean[i, lo:hi] = total
        psnd[p, 0:1, 0:rows] = sizes(total, i)
        if p == 0:
            pl.semaphore_wait(near.at[2], 2)

        @pl.loop(1, 16)
        def _(j):
            remote(psnd.at[p], prcv.at[p, j - 1], ps_s, ps_r.at[p], r, lax.rem(m + j, 16)).start()

    def rows_of(p):
        i, lo, hi = PIECES[p]
        return i, lo, hi + (16 if p == WITH_SMALL else 0)

    def ag_copy(p, d, k, group):
        i, lo, hi = rows_of(p)
        b = g.at[i, 2 * d + c, lo:hi]
        return remote(b, b, ag_s.at[p], ag_r.at[p, group], 2 * to_chip(k) + c)

    def relay_copy(p, d):
        i, lo, hi = rows_of(p)
        b = g.at[i, 2 * d + c, lo:hi]
        return remote(b, b, rl_s.at[p], rl_r.at[p], partner)

    def wait_blocks(p, n, sem):
        i, lo, hi = rows_of(p)
        wait_bytes(g.at[i, 0:n, lo:hi], sem)

    def step(p):
        i, lo, hi = PIECES[p]
        wait_bytes(prcv.at[p], ps_r.at[p])
        total = psnd[p]
        for j in range(15):
            total = total + prcv[p, j]
        ratio = jnp.sqrt(total[1:2]) * lax.rsqrt(total[0:1] + 1e-06)
        ratio = jnp.broadcast_to(ratio, (128, 128))
        if i < 3:
            ratio = jnp.transpose(ratio)[0 : hi - lo]
        state, stepped = update(mean[i, lo:hi] * ratio, mast[i, lo:hi], memo[i, lo:hi])
        g[i, r, lo:hi] = stepped.astype(BF16)
        sta[i, lo:hi] = state
        stp[i, lo:hi] = stepped

        for group, (first, last) in ((2, (5, 8)), (1, (4, 5)), (0, (1, 4))):
            if group == 2 and GATHERS[p] != "direct":
                continue

            @pl.loop(first, last)
            def _(k):
                ag_copy(p, chip, k, group).start()

        relay_copy(p, chip).start()

    def arrive(p, group):
        wait_blocks(p, (3, 1, 3)[group], ag_r.at[p, group])

    def pass_on(p, group):
        first, last = ((1, 4), (4, 5), (5, 8))[group]

        @pl.loop(first, last)
        def _(k):
            relay_copy(p, from_chip(k)).start()

    def forward(p):
        if GATHERS[p] == "z first":
            arrive(p, 1)

            @pl.loop(1, 4)
            def _(k):
                ag_copy(p, from_chip(4), k, 2).start()

            pass_on(p, 1)
        if GATHERS[p] == "y first":
            arrive(p, 0)

            @pl.loop(1, 4)
            def _(k):
                ag_copy(p, from_chip(k), 4, 2).start()

            pass_on(p, 0)

    def relay(p):
        for group in (0, 1, 2):
            if group == {"z first": 1, "y first": 0, "direct": None}[GATHERS[p]]:
                continue
            arrive(p, group)
            pass_on(p, group)

    def step_small():
        wait_bytes(sm_rcv, smr_r)
        total = sm_snd[r]
        for k in range(7):
            total = total + sm_rcv[k]
        total = total * 0.25
        rows = []
        for n in range(2):
            state, stepped = update(total[n : n + 1], sm_mast[n], sm_memo[n])
            sm_sta[n] = state
            sm_stp[n] = stepped
            rows.append(stepped)
        g[0, r, 128:144] = jnp.concatenate(rows + [jnp.zeros((14, 128), F32)], axis=0).astype(BF16)

    code(0, True)
    pl.semaphore_wait(near.at[0], 2)
    tell(x_peer, 1)
    send_small()
    code(1, True)
    prepare()
    code(2, True)
    code(3, True)
    code(4, False)
    code(5, False)
    code(6, False)
    add_up(0)
    send(4)
    add_up(1)
    send(5)
    add_up(2)
    send(6)
    step_small()
    add_up(3)
    add_up(4)
    add_up(5)
    step(0)
    add_up(6)
    step(1)
    step(2)
    step(3)
    step(4)
    forward(1)
    forward(2)
    step(5)
    relay(0)
    step(6)
    relay(1)
    relay(2)
    relay(3)
    relay(4)
    relay(5)
    relay(6)

    for p in range(7):
        wait_blocks(p, 8, rl_r.at[p])
        if p == WITH_SMALL:
            for n in range(2):
                rows = [g[0, b, 128:144].astype(F32)[n : n + 1] for b in range(16)]
                sm_g[n] = jnp.concatenate(rows, axis=0).astype(BF16)

    for i in range(4):
        wait_bytes(pair.at[i], pair_s.at[i])
    for p, (i, lo, hi) in enumerate(PIECES):
        wait_bytes(snd.at[p, :, 0 : hi - lo + 8], rs_s.at[p])
        wait_blocks(p, 7, ag_s.at[p])
        wait_blocks(p, 8, rl_s.at[p])
    wait_bytes(sm_pair, smp_s)
    wait_bytes(sm_rcv, smr_s)
    wait_bytes(prcv, ps_s)


def finish(g, stp, sta, sm_g, sm_stp, sm_sta, *rest):
    outs, sem = rest[:18], rest[18]
    pairs = [(g.at[i, :, 0:128], outs[i]) for i in range(3)]
    pairs += [(g.at[3, b, 0:128], outs[3].at[:, 128 * b : 128 * b + 128]) for b in range(16)]
    pairs += [(sm_g.at[n], outs[4 + n]) for n in range(2)]
    pairs += [(stp.at[i], outs[6 + i]) for i in range(4)] + [(sm_stp.at[n], outs[10 + n]) for n in range(2)]
    pairs += [(sta.at[i], outs[12 + i]) for i in range(4)] + [(sm_sta.at[n], outs[16 + n]) for n in range(2)]
    for src, dst in pairs:
        pltpu.make_async_copy(src, dst, sem).start()
    for src, dst in pairs:
        pltpu.make_async_copy(src, dst, sem).wait()


def shards(*args):
    partials, masters, memories = args[0:6], args[6:12], args[12:18]
    line = lambda a: a.reshape(1, 128)
    operands = (
        *[a.reshape(8, 2, 128, 128) for a in partials[0:3]],
        partials[3].reshape(128, 2048),
        partials[4], partials[5],
        *masters[0:4], *map(line, masters[4:6]),
        *memories[0:4], *map(line, memories[4:6]),
    )
    block = jax.ShapeDtypeStruct((128, 128), F32)
    row = jax.ShapeDtypeStruct((1, 128), F32)
    out_shape = (
        *[jax.ShapeDtypeStruct((16, 128, 128), BF16)] * 3,
        jax.ShapeDtypeStruct((128, 2048), BF16),
        *[jax.ShapeDtypeStruct((16, 128), BF16)] * 2,
        *[block] * 4, *[row] * 2,
        *[block] * 4, *[row] * 2,
    )
    vmem, dma = pltpu.VMEM, pltpu.SemaphoreType.DMA
    held_shape = [
        ((4, 16, 144, 128), BF16), ((4, 128, 128), F32), ((4, 128, 128), F32),
        ((2, 16, 128), BF16), ((2, 1, 128), F32), ((2, 1, 128), F32),
    ]
    held = pl.pallas_call(
        kernel,
        out_shape=[vmem(*a) for a in held_shape],
        in_specs=[pl.BlockSpec(memory_space=pltpu.HBM)] * 18,
        out_specs=[pl.BlockSpec(memory_space=pltpu.VMEM)] * 6,
        scratch_shapes=[
            vmem((4, 8, 2, 128, 128), F32), vmem((4, 8, 128, 128), F32),
            vmem((7, 7, 136, 128), BF16), vmem((7, 7, 136, 128), BF16),
            vmem((4, 128, 128), F32), vmem((4, 128, 128), F32), vmem((4, 128, 128), F32),
            vmem((2, 1, 2048), F32), vmem((2, 1, 2048), F32),
            vmem((16, 2, 128), F32), vmem((7, 2, 128), F32),
            vmem((2, 1, 128), F32), vmem((2, 1, 128), F32),
            vmem((7, 2, 128), F32), vmem((7, 15, 2, 128), F32),
            dma((4,)), dma((5,)), dma((4,)), dma((8,)), dma((3,)), dma, dma, dma, dma,
            dma((7,)), dma((7,)), dma, dma((7,)), pltpu.SemaphoreType.REGULAR((3,)),
            dma((7,)), dma((7, 3)), dma((7,)), dma((7,)),
        ],
        compiler_params=pltpu.CompilerParams(collective_id=0, has_side_effects=True, vmem_limit_bytes=62600 * 1024),
    )(*operands)
    outs = pl.pallas_call(
        finish,
        out_shape=out_shape,
        in_specs=[pl.BlockSpec(memory_space=pltpu.VMEM)] * 6,
        out_specs=(pl.BlockSpec(memory_space=pltpu.HBM),) * 18,
        scratch_shapes=[dma],
        compiler_params=pltpu.CompilerParams(vmem_limit_bytes=2**20),
    )(*held)
    outs = list(outs)
    for i in range(3):
        outs[i] = outs[i].reshape(2048, 128)
    for i in (4, 5):
        outs[i] = outs[i].reshape(2048)
    for i in (10, 11, 16, 17):
        outs[i] = outs[i].reshape(128)
    return tuple(outs)


def solution(mesh):
    col, row = P("replica", "model"), P("model", "replica")
    per = P("replica")
    return jax.shard_map(
        shards,
        mesh=mesh,
        in_specs=(
            *[P("replica", None, "model")] * 3, P("replica", "model", None), P("replica", None), P("replica", None),
            col, col, col, row, per, per,
            col, col, col, row, per, per,
        ),
        out_specs=(
            *[P(None, "model")] * 3, P("model", None), P(), P(),
            col, col, col, row, per, per,
            col, col, col, row, per, per,
        ),
        check_vma=False,
    )
```

time: 44.3 us -> 43.8 us (0.989)
  Pallas kernels: 43.5 us -> 43 us
    pallas_call x1, Pallas kernels: 42 us -> 41.5 us  [shards(): pl.pallas_call(kernel, out_shape=[vmem(*a) for a in held_shape], in_specs...]
where the time goes in v4:
time: 43.8 us; the launch traced here: 43.7 us
  Pallas kernels  43 us (98%)
  between operations  0.67 us (2%)
    pallas_call x1, Pallas kernels, shards(): pl.pallas_call(kernel, out_shape=[vmem(*a) for a in held_shape], in_specs...  41.5 us
    pallas_call x1, Pallas kernels, shards(): pl.pallas_call(finish, out_shape=out_shape, in_specs=[pl.BlockSpec(memory...  1.5 us

profile of v4, /device:TPU:1, one launch (start us, length us, event | category | flops | bytes accessed | tf_op | source)
XLA Modules:
  0.0 43.7 jit_solution(2511517899561797765)
XLA Ops:
  0.7 41.5 %shard_map.313 = (bf16[4,16,144,128]{3,2,1,0:T(8,128)(2,1)S(1)}, f32[4,128,128]{2,1,0:T(8,128)S(1)}, f32[4,128,128]{2,1,0:T(8,128)S(1)}, bf16[2,16,128]{2,1,0:T(...) custom-call(f32[8,2,128,128]{3,2,1,0:T(8,128)} %bitcast.17, f32[8,2,128,128]{3,2,1,0:T(8,128)} %bitcast.18, ...), custom_call_target="tpu_custom_call" | custom-call | tf_op jit(solution)/shard_map/pallas_call | solution.py:418
  42.2 1.5 %shard_map.314 = (bf16[16,128,128]{2,1,0:T(8,128)(2,1)}, bf16[16,128,128]{2,1,0:T(8,128)(2,1)}, bf16[16,128,128]{2,1,0:T(8,128)(2,1)}, bf16[128,2048]{1,0:T(8,12...) custom-call(bf16[4,16,144,128]{3,2,1,0:T(8,128)(2,1)S(1)} %get-tuple, ...), custom_call_target="tpu_custom_call" | custom-call | tf_op jit(solution)/shard_map/pallas_call | solution.py:437
